TPU v7x, 32 devices: a whole 2x2x4 slice. The times are simulated.
32 devices in a mesh: gx: 2 (over x), gy: 16 (over z, y, core).
Axes of the slice: x: 2, y: 2, z: 4, core: 2. Of those that a mesh axis runs over, the one named last changes fastest.
Arguments:
- cell: int32 [1048576], P(('gx', 'gy')), may hold values from 0 to 524287
- vehicle: int32 [1048576], P(('gx', 'gy')), may hold values from 0 to 1023
- speed: float32 [1048576], P(('gx', 'gy')), may hold values from 0 to 64, as said below
Outputs:
- top_speed: float32 [524288], P(('gx', 'gy'))
- top_vehicle: int32 [524288], P(('gx', 'gy'))
Inputs may be any that keep to these rules, and one draw needn't show every extreme that they name: Every speed is a whole multiple of 1/1024.
All inputs are finite; a program needn't handle non-finite values.
Results may differ from a plain program's by a relative error of at most 0.0003.
Values sent between devices are 32-bit elements; how exact they have to be, the bound alone decides.
No kernel may reach another device: no remote copies, remote signals or barrier semaphores. Data moves between devices by JAX's collectives and lax.ppermute only.
A program may use at most 64 MiB of HBM per device.

v0:
```python
import jax
import jax.numpy as jnp
from jax import lax
from jax.sharding import PartitionSpec as P

CELLS = 524288
VEHICLES = 1024


def swapped(block, axis, apart):
    count = lax.axis_size(axis)
    route = []
    for low in range(count):
        high = low | 1 << apart
        if high != low and high < count:
            route += [(low, high), (high, low)]
    return lax.ppermute(block, axis, route)


def combine(first, second):
    speed_a = first[0]
    speed_b = second[0]
    best = jnp.maximum(speed_a, speed_b)
    ident = jnp.where(
        speed_a > speed_b,
        first[1],
        jnp.where(speed_b > speed_a, second[1], jnp.minimum(first[1], second[1])),
    )
    return jnp.stack([best, ident])


def per_device(cell, vehicle, speed):
    local_best = jnp.full((CELLS,), -1.0, jnp.float32).at[cell].max(speed)
    chosen = jnp.where(speed == local_best[cell], vehicle, VEHICLES)
    local_ident = jnp.full((CELLS,), VEHICLES, jnp.int32).at[cell].min(chosen)
    paired = jnp.stack([local_best, local_ident.astype(jnp.float32)])
    outer = lax.axis_size("gx")
    inner = lax.axis_size("gy")
    nbits = (outer * inner).bit_length() - 1
    myself = lax.axis_index(("gx", "gy"))
    buffer = paired
    for level in reversed(range(nbits)):
        half = buffer.shape[1] // 2
        side = myself >> level & 1
        keep = lax.dynamic_slice_in_dim(buffer, side * half, half, 1)
        give = lax.dynamic_slice_in_dim(buffer, (1 - side) * half, half, 1)
        partner = swapped(give, ("gx", "gy"), level)
        buffer = combine(keep, partner)
    best = buffer[0]
    ident = buffer[1]
    lowest = ident.astype(jnp.int32)
    top_vehicle = jnp.where(lowest < VEHICLES, lowest, -1)
    return (best, top_vehicle)


def solution(mesh):
    placed = (P(("gx", "gy")), P(("gx", "gy")), P(("gx", "gy")))
    return jax.shard_map(
        per_device,
        mesh=mesh,
        in_specs=placed,
        out_specs=(P(("gx", "gy")), P(("gx", "gy"))),
        check_vma=False,
    )
```

profile of v0, /device:TPU:0, one launch (start us, length us, event | category | flops | bytes accessed | tf_op | source)
XLA Modules:
  0.0 671.6 jit_solution(18166627678722901278)
XLA Ops:
  0.6 0.9 broadcast_clamp_fusion
  1.6 171.8 %scatter_custom_fusion = f32[524288]{0:T(1024)S(1)} fusion(s32[32768]{0:T(1024)S(1)} %get-tuple-element.26, f32[32768]{0:T(1024)} %param.5, f32[]{:T(128)} %constant.18.clone.1), kind=kCustom, calls=%fused_computation.25 | custom fusion | flops 32768 | bytes 2097664 | tf_op jit(solution)/shard_map/scatter-max | solution.py:33
  173.4 0.0 copy-start
  173.4 0.0 copy-start.1
  173.5 180.5 %gather_fusion = f32[32768]{0:T(1024)S(1)} fusion(f32[524288]{0:T(1024)S(1)} %scatter_custom_fusion, s32[32768]{0:T(1024)S(1)} %get-tuple-element.25), kind=kCustom, calls=%fused_computation | custom fusion | bytes 393216 | tf_op jit(solution)/shard_map/gather | solution.py:34
  354.0 0.0 copy-done
  354.0 0.0 copy-done.1
  354.1 176.3 %scatter_custom_fusion.1 = s32[524288]{0:T(1024)} fusion(s32[32768]{0:T(1024)S(1)} %get-tuple-element.26, s32[32768]{0:T(1024)S(1)} %compare_select_fusion.10, s32[]{:T(128)} %constant.21.clone.1), kind=kCustom, calls=%fused_computation.23 | custom fusion | flops 32768 | bytes 2097156 | tf_op jit(solution)/shard_map/scatter-min | solution.py:35
  530.4 3.1 convert_element_type.6
  533.5 7.0 %fusion.1 = (f32[2,262144]{1,0:T(2,128)}, f32[2,262144]{1,0:T(2,128)}) fusion(s32[]{:T(128)S(6)} %select_n.88, f32[1,524288]{1,0:T(1,128)S(1)} %bitcast.5, f32[1,524288]{1,0:T(1,128)} %bitcast.6, s32[]{:T(128)S(6)} %select_n.89), kind=kLoop, calls=%fused_computation.14 | loop fusion | flops 1048576 | bytes 8388616 | tf_op jit(solution)/shard_map/stack | solution.py:36
  540.5 3.0 collective-permute-start
  543.5 45.8 %collective-permute-done = f32[2,262144]{1,0:T(2,128)S(1)} collective-permute-done((f32[2,262144]{1,0:T(2,128)}, f32[2,262144]{1,0:T(2,128)S(1)}, u32[]{:S(2)}, u32[]{:S(2)}) %collective-permute-start) | collective-permute-done | bytes 2097184 | tf_op jit(solution)/shard_map/ppermute | solution.py:17
  589.3 4.9 compare_select_fusion.1
  594.2 2.2 fusion.3
  596.5 2.9 collective-permute-start.1
  599.4 44.9 %collective-permute-done.1 = f32[2,131072]{1,0:T(2,128)S(1)} collective-permute-done((f32[2,131072]{1,0:T(2,128)S(1)}, f32[2,131072]{1,0:T(2,128)S(1)}, u32[]{:S(2)}, u32[]{:S(2)}) %collective-permute-start.1) | collective-permute-done | bytes 1048608 | tf_op jit(solution)/shard_map/ppermute | solution.py:17
  644.2 1.4 compare_select_fusion.3
  645.6 1.2 fusion.9
  646.8 0.7 collective-permute-start.2
  647.5 12.2 %collective-permute-done.2 = f32[2,65536]{1,0:T(2,128)S(1)} collective-permute-done((f32[2,65536]{1,0:T(2,128)S(1)}, f32[2,65536]{1,0:T(2,128)S(1)}, u32[]{:S(2)}, u32[]{:S(2)}) %collective-permute-start.2) | collective-permute-done | bytes 524320 | tf_op jit(solution)/shard_map/ppermute | solution.py:17
  659.7 0.7 compare_select_fusion.5
  660.4 0.6 fusion.11
  661.0 1.5 collective-permute-start.3
  662.5 5.1 collective-permute-done.3
  667.6 0.3 compare_select_fusion.7
  667.9 0.3 fusion.13
  668.3 0.1 collective-permute-start.4
  668.4 1.3 collective-permute-done.4
  669.7 0.4 compare_reduce_fusion
  670.1 0.8 fusion.16
  670.9 0.7 compare_select_fusion.9
  (1 shorter events, 0.0 us)
Async XLA Ops:
  173.4 180.6 %copy-start = (f32[32768]{0:T(1024)S(1)}, f32[32768]{0:T(1024)}, u32[]{:S(2)}) copy-start(f32[32768]{0:T(1024)} %param.5) | copy-start | bytes 393220
  173.4 180.6 %copy-start.1 = (s32[32768]{0:T(1024)S(1)}, s32[32768]{0:T(1024)}, u32[]{:S(2)}) copy-start(s32[32768]{0:T(1024)} %param.4) | copy-start | bytes 393220
  540.5 48.8 %collective-permute-start = (f32[2,262144]{1,0:T(2,128)}, f32[2,262144]{1,0:T(2,128)S(1)}, u32[]{:S(2)}, u32[]{:S(2)}) collective-permute-start(f32[2,262144]{1,0:T(2,128)} %get-tuple-element.7), channel_id=1, source_target_pairs={{0,16},{16,0},{1,17},{17,1},{2,18},{18,2},{3,19},{19,3},{4,20},{20... | collective-permute-start | bytes 6291464 | tf_op jit(solution)/shard_map/ppermute | solution.py:17
  596.5 47.8 %collective-permute-start.1 = (f32[2,131072]{1,0:T(2,128)S(1)}, f32[2,131072]{1,0:T(2,128)S(1)}, u32[]{:S(2)}, u32[]{:S(2)}) collective-permute-start(f32[2,131072]{1,0:T(2,128)S(1)} %get-tuple-element.11), channel_id=1, source_target_pairs={{0,8},{8,0},{1,9},{9,1},{2,10},{10,2},{3,11},{11,3},{4,12},{12,4},... | collective-permute-start | bytes 3145736 | tf_op jit(solution)/shard_map/ppermute | solution.py:17
  646.8 12.9 %collective-permute-start.2 = (f32[2,65536]{1,0:T(2,128)S(1)}, f32[2,65536]{1,0:T(2,128)S(1)}, u32[]{:S(2)}, u32[]{:S(2)}) collective-permute-start(f32[2,65536]{1,0:T(2,128)S(1)} %get-tuple-element.15), channel_id=1, source_target_pairs={{0,4},{4,0},{1,5},{5,1},{2,6},{6,2},{3,7},{7,3},{8,12},{12,8},{9,1... | collective-permute-start | bytes 1572872 | tf_op jit(solution)/shard_map/ppermute | solution.py:17
  661.0 6.6 collective-permute-start.3
  668.3 1.4 collective-permute-start.4
where the time goes:
time: 672 us
  other arithmetic  373 us (56%)
  local copies, waits for them, and re-layouts  181 us (27%)
  waiting for transfers between devices  109 us (16%)
  starting transfers between devices  8.18 us (1%)
    gather x1, local copies, waits for them, and re-layouts, per_device(): chosen = jnp.where(speed == local_best[cell], vehicle, VEHICLES)  181 us
    another operation x1, other arithmetic, per_device(): local_ident = jnp.full((CELLS,), VEHICLES, jnp.int32).at[cell].min(chosen)  176 us
    another operation x1, other arithmetic, per_device(): local_best = jnp.full((CELLS,), -1.0, jnp.float32).at[cell].max(speed)  172 us
    ppermute x5, waiting for transfers between devices, swapped(): return lax.ppermute(block, axis, route)  109 us
  transfers between devices with their start and end apart: 5, of which 5 were waited for; matrix products, arithmetic and copies ran while one was open for 0% of the time, Pallas kernels for 0%

commit v1 on v0

v1 whole, which is shorter than its diff:
```python
import functools

import jax
import jax.numpy as jnp
from jax import lax
from jax.experimental import pallas as pl
from jax.experimental.pallas import tpu as pltpu
from jax.sharding import PartitionSpec as P

CELLS = 524288
VEHICLES = 1024
STEPS = 1024
AXES = ("gx", "gy")
LANES = 128
ROWS = 8
TILE = ROWS * LANES
BLOCK = LANES * LANES
CUT = 15
LOW = (1 << CUT) - 1


def sub_iota():
    return lax.broadcasted_iota(jnp.int32, (ROWS, LANES), 0)


def lane_iota():
    return lax.broadcasted_iota(jnp.int32, (ROWS, LANES), 1)


def turned(regs):
    out = []
    for first in range(0, len(regs), 16):
        block = jnp.concatenate(regs[first : first + 16], axis=0).T
        out += [block[ROWS * i : ROWS * (i + 1)] for i in range(16)]
    return out


def place(bit, linear):
    if bit >= 14:
        return "v", bit - 10
    if linear:
        return ("l", bit) if bit < 7 else ("s", bit - 7) if bit < 10 else ("v", bit - 10)
    return ("s", bit) if bit < 3 else ("v", bit - 3) if bit < 7 else ("l", bit - 7)


def flip(regs, bit, linear):
    kind, at = place(bit, linear)
    if kind == "v":
        return [~x if g >> at & 1 else x for g, x in enumerate(regs)]
    index = sub_iota() if kind == "s" else lane_iota()
    mask = -((index >> at) & 1)
    return [x ^ mask for x in regs]


def exchange(keys, loads, bit, linear):
    kind, at = place(bit, linear)
    keys, loads = list(keys), list(loads)
    if kind == "v":
        for low in range(len(keys)):
            high = low | 1 << at
            if high == low:
                continue
            a, b, p, q = keys[low], keys[high], loads[low], loads[high]
            swap = a > b
            keys[low], keys[high] = jnp.minimum(a, b), jnp.maximum(a, b)
            loads[low], loads[high] = jnp.where(swap, q, p), jnp.where(swap, p, q)
        return keys, loads
    step = 1 << at
    upper = (sub_iota() >> at & 1) == 1

    def partner(x):
        if 2 * step == ROWS:
            return pltpu.roll(x, step, 0)
        return jnp.where(upper, pltpu.roll(x, step, 0), pltpu.roll(x, ROWS - step, 0))

    for g, (a, p) in enumerate(zip(keys, loads)):
        b, q = partner(a), partner(p)
        new = jnp.where(upper, jnp.maximum(a, b), jnp.minimum(a, b))
        keys[g], loads[g] = new, jnp.where(new == a, p, q)
    return keys, loads


def sort_pairs(keys, loads, first_level, linear):
    bits = (len(keys) * TILE).bit_length() - 1
    for level in range(first_level, bits + 1):
        if level > first_level:
            keys = flip(keys, level - 1, linear)
        if level < bits:
            keys = flip(keys, level, linear)
        for bit in reversed(range(level)):
            if bit < 14 and linear != (bit >= 7):
                keys, loads, linear = turned(keys), turned(loads), not linear
            keys, loads = exchange(keys, loads, bit, linear)
    assert not linear
    return keys, loads


def lane_next(regs, fill):
    rolled = [pltpu.roll(x, LANES - 1, 1) for x in regs]
    rolled.append(jnp.full_like(rolled[0], fill))
    last = lane_iota() == LANES - 1
    return [jnp.where(last, rolled[h + 1], rolled[h]) for h in range(len(regs))]


def pull(regs, bit, linear):
    count = len(regs)
    blocks = count // 16
    kind, at = place(bit, linear)
    zero = jnp.zeros_like(regs[0])
    if kind == "s":
        step = 1 << at
        rolled = [pltpu.roll(x, ROWS - step, 0) for x in regs]
        stay = sub_iota() < ROWS - step
        if linear:
            over = rolled[1:] + [zero]
        else:
            wrap = lane_next([rolled[16 * h] for h in range(blocks)], 0)
            over = [rolled[g + 1] if (g + 1) % 16 else wrap[g // 16] for g in range(count)]
        return [jnp.where(stay, a, b) for a, b in zip(rolled, over)]
    step = 1 << at
    if linear or step >= 16:
        return regs[step:] + [zero] * step
    out = [None] * count
    for v in range(16):
        if v + step < 16:
            for h in range(blocks):
                out[16 * h + v] = regs[16 * h + v + step]
        else:
            wrap = lane_next([regs[16 * h + v + step - 16] for h in range(blocks)], 0)
            for h in range(blocks):
                out[16 * h + v] = wrap[h]
    return out


def push(regs, bit, linear):
    assert len(regs) == 16
    kind, at = place(bit, linear)
    zero = jnp.zeros_like(regs[0])
    first = lane_iota() == 0

    def lane_last(x):
        return jnp.where(first, 0, pltpu.roll(x, 1, 1))

    step = 1 << at
    if kind == "s":
        rolled = [pltpu.roll(x, step, 0) for x in regs]
        over = [zero if linear else lane_last(rolled[15])] + rolled[:15]
        stay = sub_iota() >= step
        return [jnp.where(stay, a, b) for a, b in zip(rolled, over)]
    head = [zero] * step if linear else [lane_last(x) for x in regs[16 - step :]]
    return head + regs[: 16 - step]


def spread_row(x, row):
    return jnp.broadcast_to(x[row : row + 1], (ROWS, LANES))


def down_lanes(row):
    return turned([row] * 16)


def over_rows(regs, op):
    while len(regs) > 1:
        regs = [op(a, b) for a, b in zip(regs[0::2], regs[1::2])]
    x = regs[0]
    for step in (4, 2, 1):
        x = op(x, pltpu.roll(x, step, 0))
    return x


def run_max(cells, keys):
    count = len(cells)
    blocks = count // 16
    sub = sub_iota()
    keys = list(keys)
    for step in (1, 2, 4):
        inside = sub >= step
        for g in range(count):
            same = (pltpu.roll(cells[g], step, 0) == cells[g]) & inside
            keys[g] = jnp.where(same, jnp.maximum(keys[g], pltpu.roll(keys[g], step, 0)), keys[g])
    for h in range(blocks):
        for v in range(1, 16):
            g = 16 * h + v
            cell, key = spread_row(cells[g - 1], 7), spread_row(keys[g - 1], 7)
            keys[g] = jnp.where(cells[g] == cell, jnp.maximum(keys[g], key), keys[g])
    last_cell = [spread_row(cells[16 * h + 15], 7) for h in range(blocks)]
    last_key = [spread_row(keys[16 * h + 15], 7) for h in range(blocks)]
    rolled = [jnp.full((ROWS, LANES), -9, jnp.int32)] + [pltpu.roll(x, 1, 1) for x in last_cell]
    lane = lane_iota()
    before = [jnp.where(lane == 0, rolled[h], rolled[h + 1]) for h in range(blocks)]
    cell_col = [down_lanes(x) for x in last_cell]
    key_col = [down_lanes(x) for x in last_key]
    for h in range(blocks):
        terms = []
        for source in range(h + 1):
            for v in range(16):
                match = cell_col[source][v] == before[h]
                if source == h:
                    match = match & (sub + ROWS * v < lane)
                terms.append((match, key_col[source][v]))
        terms = [jnp.where(match, key, -1) for match, key in terms]
        while len(terms) % 16 or len(terms) & (len(terms) - 1):
            terms.append(terms[0])
        best = over_rows(terms, jnp.maximum)
        for g in range(16 * h, 16 * h + 16):
            keys[g] = jnp.where(cells[g] == before[h], jnp.maximum(keys[g], best), keys[g])
    return keys


def run_ends(cells):
    count = len(cells)
    rolled = [pltpu.roll(x, ROWS - 1, 0) for x in cells]
    wrap = lane_next([rolled[16 * h] for h in range(count // 16)], -9)
    over = [rolled[g + 1] if (g + 1) % 16 else wrap[g // 16] for g in range(count)]
    bottom = sub_iota() == ROWS - 1
    return [c != jnp.where(bottom, b, a) for c, a, b in zip(cells, rolled, over)]


def ranks(flags):
    count = len(flags)
    blocks = count // 16
    sub, lane = sub_iota(), lane_iota()
    out, total = [], jnp.zeros((ROWS, LANES), jnp.int32)
    for h in range(blocks):
        sums, run = [], jnp.zeros((ROWS, LANES), jnp.int32)
        for v in range(16):
            flag = flags[16 * h + v]
            x = flag
            for step in (1, 2, 4):
                x = x + jnp.where(sub >= step, pltpu.roll(x, step, 0), 0)
            sums.append(x - flag + run)
            run = run + spread_row(x, 7)
        col = down_lanes(run)
        start = [jnp.where(sub + ROWS * v < lane, col[v], 0) for v in range(16)]
        start = over_rows(start, jnp.add) + total
        total = total + over_rows(col, jnp.add)
        out += [x + start for x in sums]
    return out, total


def positions(count, linear):
    sub, lane = sub_iota(), lane_iota()
    if linear:
        return [TILE * g + LANES * sub + lane for g in range(count)]
    return [BLOCK * (g // 16) + LANES * lane + ROWS * (g % 16) + sub for g in range(count)]


def travel(move, load, bit, linear, shift, empty):
    probe = 1 << (CUT + bit)
    new_move, new_load = shift(move, bit, linear), shift(load, bit, linear)
    for g in range(len(move)):
        arrives = (new_move[g] & probe) != 0
        leaves = (move[g] & probe) != 0
        stay = load[g] if empty is None else jnp.where(leaves, empty, load[g])
        new_move[g] = jnp.where(arrives, new_move[g], jnp.where(leaves, 0, move[g]))
        new_load[g] = jnp.where(arrives, new_load[g], stay)
    return new_move, new_load


def compact(cells, keys, wanted):
    count = len(cells)
    rank, total = ranks([jnp.where(w, 1, 0) for w in wanted])
    at = positions(count, False)
    move = [
        jnp.where(w, (i - r) << CUT | c, 0) for w, i, r, c in zip(wanted, at, rank, cells)
    ]
    for bit in range((count * TILE).bit_length() - 1):
        if bit == 7:
            move, keys = turned(move), turned(keys)
        move, keys = travel(move, keys, bit, bit >= 7, pull, None)
    return [x & LOW for x in move], keys, total


def split_kernel(own, slots, chunk, round_ref, odd_ref, cell_ref, vehicle_ref, speed_ref, out_ref, low_ref, high_ref):
    n = CELLS // own
    count = cell_ref.shape[0] // ROWS
    odd = odd_ref[0]
    cells, keys = [], []
    for g in range(count):
        at = pl.ds(ROWS * g, ROWS)
        cell = cell_ref[at, :]
        cells.append(jnp.where(odd == 1, CELLS - 1 - cell, cell))
        level = (speed_ref[at, :] * float(STEPS)).astype(jnp.int32)
        keys.append(level * VEHICLES + (VEHICLES - 1 - vehicle_ref[at, :]))
    cells, keys = sort_pairs(cells, keys, 1, False)
    keys = run_max(cells, keys)
    ends = run_ends(cells)
    shift = own.bit_length() - 1
    owner = [jnp.where(w, c >> shift, -1) for w, c in zip(ends, cells)]
    high = [k | (c >> CUT) << 27 for k, c in zip(keys, cells)]
    low, high, _ = compact([c & LOW for c in cells], high, ends)
    for g in range(count):
        at = pl.ds(ROWS * g, ROWS)
        low_ref[at, :] = low[g]
        high_ref[at, :] = high[g]
    low_ref[pl.ds(ROWS * count, ROWS), :] = jnp.zeros((ROWS, LANES), jnp.int32)
    high_ref[pl.ds(ROWS * count, ROWS), :] = jnp.zeros((ROWS, LANES), jnp.int32)
    sizes = [jnp.sum(sum(jnp.where(w == o, 1, 0) for w in owner)) for o in range(n)]
    most = functools.reduce(jnp.maximum, sizes)
    sub, lane = sub_iota(), lane_iota()
    skip = round_ref[0] * (slots * LANES)
    base = jnp.int32(0)
    for o in range(n):
        start = base + skip
        valid = sub * LANES + lane < sizes[o] - skip
        start = jnp.minimum(start, count * TILE)
        base = base + sizes[o]
        row, off = start >> 7, start & 127

        def window(ref):
            x = pltpu.roll(ref[pl.ds(row, ROWS), :], (LANES - off) & 127, 1)
            return jnp.where(lane < LANES - off, x, pltpu.roll(x, ROWS - 1, 0))

        low_w, high_w = window(low_ref), window(high_ref)
        cell = jnp.where(valid, low_w & (own - 1), own).astype(jnp.float32)
        key = jnp.where(valid, high_w & ((1 << 27) - 1), 0)
        speed = (key >> 10).astype(jnp.float32) * (1.0 / STEPS)
        ident = (VEHICLES - 1 - (key & (VEHICLES - 1))).astype(jnp.float32)
        target = pl.multiple_of(jnp.where(odd == 1, n - 1 - o, o) * chunk, chunk)
        for w, x in enumerate((cell, speed, ident)):
            out_ref[pl.ds(target + w * slots, slots), :] = x[:slots]
        tail = chunk - 3 * slots
        fill = jnp.full((tail, LANES), most.astype(jnp.float32))
        out_ref[pl.ds(target + 3 * slots, tail), :] = fill


def join_kernel(own, n, slots, chunk, in_ref, speed_ref, ident_ref, most_ref):
    sub = sub_iota()
    per = ROWS // run_rows(slots)
    cells, keys = [], []
    most = jnp.zeros((1, LANES), jnp.float32)
    for g in range(n // per):
        if per == 1:
            part = [in_ref[pl.ds(chunk * g + w * slots, slots), :] for w in range(3)]
            pad = jnp.zeros((ROWS - slots, LANES), jnp.float32)
            part = [jnp.concatenate([x, pad], axis=0) for x in part]
            live = sub < slots
            source = g & 1
        else:
            part = [in_ref[pl.ds(chunk * per * g + w, ROWS, stride=chunk), :] for w in range(3)]
            live = sub >= 0
            source = sub & 1
        for k in range(per):
            most = jnp.maximum(most, in_ref[pl.ds(chunk * (per * g + k + 1) - 1, 1), :])
        cell = jnp.where(live, part[0].astype(jnp.int32), own)
        if per == 1:
            cell = own - 1 - cell if source else cell
        else:
            cell = jnp.where(source == 1, own - 1 - cell, cell)
        level = (part[1] * float(STEPS)).astype(jnp.int32)
        cells.append(cell)
        keys.append(level * VEHICLES + (VEHICLES - 1 - part[2].astype(jnp.int32)))
    most_ref[...] = most
    first = (run_rows(slots) * LANES).bit_length()
    cells, keys = sort_pairs(cells, keys, first, True)
    keys = run_max(cells, keys)
    ends = [w & (c >= 0) & (c < own) for w, c in zip(run_ends(cells), cells)]
    cells, keys, total = compact(cells, keys, ends)
    keep = max(own // TILE, 1)
    at = positions(16, True)
    move = [jnp.where(i < total, (c - i) << CUT, 0) for i, c in zip(at, cells)]
    keys = [jnp.where(i < total, k, -1) for i, k in zip(at, keys)]
    linear = True
    for bit in reversed(range(own.bit_length() - 1)):
        if bit == 6:
            move, keys, linear = turned(move), turned(keys), False
        move, keys = travel(move, keys, bit, linear, push, -1)
    keys = turned(keys)
    for g in range(keep):
        key = keys[g]
        at = pl.ds(ROWS * g, ROWS)
        speed = (key >> 10).astype(jnp.float32) * (1.0 / STEPS)
        speed_ref[at, :] = jnp.where(key >= 0, speed, -1.0)
        ident_ref[at, :] = jnp.where(key >= 0, VEHICLES - 1 - (key & (VEHICLES - 1)), -1)


def run_rows(slots):
    return 1 << (slots - 1).bit_length()


def per_device(cell, vehicle, speed):
    n = lax.axis_size(AXES)
    own = CELLS // n
    events = cell.shape[0]
    slots = max(1, (5 * events // n) // (8 * LANES))
    chunk = -(-(3 * slots + 1) // ROWS) * ROWS
    rows = events // LANES
    smem = pl.BlockSpec(memory_space=pltpu.SMEM)
    vmem = pl.BlockSpec(memory_space=pltpu.VMEM)
    table = (own // LANES, LANES)
    odd = (lax.axis_index(AXES) & 1).reshape(1)
    inputs = [x.reshape(rows, LANES) for x in (cell, vehicle, speed)]

    split = pl.pallas_call(
        functools.partial(split_kernel, own, slots, chunk),
        out_shape=jax.ShapeDtypeStruct((n * chunk, LANES), jnp.float32),
        in_specs=[smem, smem, vmem, vmem, vmem],
        out_specs=vmem,
        scratch_shapes=[pltpu.VMEM((rows + ROWS, LANES), jnp.int32)] * 2,
        name="split",
    )
    join = pl.pallas_call(
        functools.partial(join_kernel, own, n, slots, chunk),
        out_shape=(
            jax.ShapeDtypeStruct(table, jnp.float32),
            jax.ShapeDtypeStruct(table, jnp.int32),
            jax.ShapeDtypeStruct((1, LANES), jnp.float32),
        ),
        in_specs=[vmem],
        out_specs=(vmem, vmem, vmem),
        name="join",
    )

    def one_round(index):
        sent = split(index.reshape(1), odd, *inputs)
        got = lax.all_to_all(sent.reshape(n, chunk, LANES), AXES, 0, 0, tiled=True)
        return join(got.reshape(n * chunk, LANES))

    best, ident, most = one_round(jnp.int32(0))
    rounds = -(-most[0, 0].astype(jnp.int32) // (slots * LANES))

    def again(state):
        index, best, ident = state
        more, other, _ = one_round(index)
        ident = jnp.where(
            more > best, other, jnp.where(more < best, ident, jnp.minimum(ident, other))
        )
        return index + 1, jnp.maximum(best, more), ident

    _, best, ident = lax.while_loop(
        lambda state: state[0] < rounds, again, (jnp.int32(1), best, ident)
    )
    return best.reshape(own), ident.reshape(own)


def solution(mesh):
    placed = P(AXES)
    return jax.shard_map(
        per_device,
        mesh=mesh,
        in_specs=(placed, placed, placed),
        out_specs=(placed, placed),
        check_vma=False,
    )
```

time: 672 us -> 34.4 us (0.05)
  other arithmetic: 373 us -> 0 us
  local copies, waits for them, and re-layouts: 181 us -> 2 us
  waiting for transfers between devices: 109 us -> 10.3 us
  Pallas kernels: 0 us -> 13.6 us
    another operation x7 -> x0, other arithmetic: 360 us -> none  [the longest x1 176 us: per_device(): local_ident = jnp.full((CELLS,), VEHICLES, jnp.int32).at[cell].min(chosen)]
    gather x1 -> x0, local copies, waits for them, and re-layouts: 181 us -> none  [per_device(): chosen = jnp.where(speed == local_best[cell], vehicle, VEHICLES)]
    ppermute x5 -> x0, waiting for transfers between devices: 109 us -> none  [swapped(): return lax.ppermute(block, axis, route)]
    pallas_call x0 -> x2, Pallas kernels: none -> 13.6 us  [the longest x1 8.22 us: one_round(): sent = split(index.reshape(1), odd, *inputs)]
    all_to_all x0 -> x1, waiting for transfers between devices: none -> 10.3 us  [one_round(): got = lax.all_to_all(sent.reshape(n, chunk, LANES), AXES, 0, 0, tiled=True)]
    ppermute x5 -> x0, starting transfers between devices: 8.18 us -> none  [swapped(): return lax.ppermute(block, axis, route)]
    select_n x6 -> x0, other arithmetic: 7.96 us -> none  [the longest x4 7.28 us: combine(): jnp.where(speed_a > speed_b, first[1], jnp.where(speed_b > speed_a, secon...]
    all_to_all x0 -> x1, starting transfers between devices: none -> 7.33 us  [one_round(): got = lax.all_to_all(sent.reshape(n, chunk, LANES), AXES, 0, 0, tiled=True)]
  transfers between devices with their start and end apart: 5 -> 1, of which waited for: 5 -> 1; matrix products, arithmetic and copies ran while one was open for 0% -> 0% of each run, Pallas kernels for 0% -> 0%
where the time goes in v1:
time: 34.4 us; the launch traced here: 34.2 us
  Pallas kernels  13.6 us (40%)
  waiting for transfers between devices  10.3 us (30%)
  starting transfers between devices  7.33 us (21%)
  local copies, waits for them, and re-layouts  2 us (6%)
  between operations  0.76 us (2%)
    all_to_all x1, waiting for transfers between devices, one_round(): got = lax.all_to_all(sent.reshape(n, chunk, LANES), AXES, 0, 0, tiled=True)  10.3 us
    pallas_call x1, Pallas kernels, one_round(): sent = split(index.reshape(1), odd, *inputs)  8.22 us
    all_to_all x1, starting transfers between devices, one_round(): got = lax.all_to_all(sent.reshape(n, chunk, LANES), AXES, 0, 0, tiled=True)  7.33 us
    pallas_call x1, Pallas kernels, one_round(): return join(got.reshape(n * chunk, LANES))  5.41 us
    unnamed x14, local copies, waits for them, and re-layouts  2 us
  transfers between devices with their start and end apart: 1, of which 1 were waited for; matrix products, arithmetic and copies ran while one was open for 0% of the time, Pallas kernels for 0%

profile of v1, /device:TPU:0, one launch (start us, length us, event | category | flops | bytes accessed | tf_op | source)
XLA Modules:
  0.0 34.2 jit_solution(2003814703227046915)
XLA Ops:
  0.6 8.2 %split.2 = f32[512,128]{1,0:T(8,128)} custom-call(s32[1]{0:T(128)} %constant.23.clone.1.round_ref, s32[1]{0:T(128)} %bitcast.3.odd_ref, s32[256,128]{1,0:T(8,128)} %bitcast.23, s32[256,128]{1,0:T(8,128)} %bitcast.25, f32[256,128]{1,0:T(8,128)} %bitcast.27), custom_call_target="tpu_custom_call" | custom-call | tf_op jit(solution)/shard_map/split/pallas_call | solution.py:415
  8.9 0.0 copy-start.5
  8.9 7.3 %all-to-all-start.1 = ((f32[32,16,128]{2,1,0:T(8,128)}), f32[32,16,128]{2,1,0:T(8,128)S(1)}, u32[]{:S(2)}, u32[]{:S(2)}) async-start(f32[32,16,128]{2,1,0:T(8,128)} %bitcast.30), calls=%async_computation.1 | async-start | bytes 524288 | tf_op jit(solution)/shard_map/all_to_all | solution.py:416
  16.2 10.3 %all-to-all-done.1 = f32[32,16,128]{2,1,0:T(8,128)S(1)} async-done(((f32[32,16,128]{2,1,0:T(8,128)}), f32[32,16,128]{2,1,0:T(8,128)S(1)}, u32[]{:S(2)}, u32[]{:S(2)}) %all-to-all-start.1) | async-done | bytes 262176 | tf_op jit(solution)/shard_map/all_to_all | solution.py:416
  26.4 0.0 copy-start.7
  26.5 0.7 %copy-done.7 = f32[32,16,128]{2,1,0:T(8,128)} copy-done((f32[32,16,128]{2,1,0:T(8,128)}, f32[32,16,128]{2,1,0:T(8,128)S(1)}, u32[]{:S(2)}) %copy-start.7) | copy-done | bytes 262168
  27.1 0.0 copy-start.3
  27.2 0.0 copy-start.4
  27.2 5.4 %join.2 = (f32[128,128]{1,0:T(8,128)S(1)}, s32[128,128]{1,0:T(8,128)S(1)}, f32[1,128]{1,0:T(1,128)}) custom-call(f32[512,128]{1,0:T(8,128)} %bitcast.31), custom_call_target="tpu_custom_call" | custom-call | tf_op jit(solution)/shard_map/join/pallas_call | solution.py:417
  32.6 0.0 copy-start.8
  32.6 0.7 %copy-done.8 = f32[1,128]{1,0:T(1,128)S(1)} copy-done((f32[1,128]{1,0:T(1,128)S(1)}, f32[1,128]{1,0:T(1,128)}, u32[]{:S(2)}) %copy-start.8) | copy-done | bytes 536
  33.3 0.0 copy-done.5
  33.3 0.0 copy-done.3
  33.3 0.0 copy-done.4
  33.3 0.2 while.12
  33.5 0.0 copy-start.1
  33.5 0.0 copy-start.6
  33.5 0.6 %copy-done.1 = f32[128,128]{1,0:T(8,128)} copy-done((f32[128,128]{1,0:T(8,128)}, f32[128,128]{1,0:T(8,128)S(1)}, u32[]{:S(2)}) %copy-start.1) | copy-done | bytes 65560
  34.1 0.0 copy-done.6
Async XLA Ops:
  8.9 24.4 %copy-start.5 = (f32[32768]{0:T(1024)S(1)}, f32[32768]{0:T(1024)}, u32[]{:S(2)}) copy-start(f32[32768]{0:T(1024)} %param.7) | copy-start | bytes 393220
  8.9 17.6 %all-to-all-start.1 = ((f32[32,16,128]{2,1,0:T(8,128)}), f32[32,16,128]{2,1,0:T(8,128)S(1)}, u32[]{:S(2)}, u32[]{:S(2)}) async-start(f32[32,16,128]{2,1,0:T(8,128)} %bitcast.30), calls=%async_computation.1 | async-start | bytes 524288 | tf_op jit(solution)/shard_map/all_to_all | solution.py:416
  26.4 0.7 %copy-start.7 = (f32[32,16,128]{2,1,0:T(8,128)}, f32[32,16,128]{2,1,0:T(8,128)S(1)}, u32[]{:S(2)}) copy-start(f32[32,16,128]{2,1,0:T(8,128)S(1)} %all-to-all-done.1) | copy-start | bytes 786436
  27.1 6.1 %copy-start.3 = (s32[32768]{0:T(1024)S(1)}, s32[32768]{0:T(1024)}, u32[]{:S(2)}) copy-start(s32[32768]{0:T(1024)} %param.5) | copy-start | bytes 393220
  27.2 6.2 %copy-start.4 = (s32[32768]{0:T(1024)S(1)}, s32[32768]{0:T(1024)}, u32[]{:S(2)}) copy-start(s32[32768]{0:T(1024)} %param.6) | copy-start | bytes 393220
  32.6 0.7 %copy-start.8 = (f32[1,128]{1,0:T(1,128)S(1)}, f32[1,128]{1,0:T(1,128)}, u32[]{:S(2)}) copy-start(f32[1,128]{1,0:T(1,128)} %get-tuple-element.53) | copy-start | bytes 1540
  33.5 0.6 %copy-start.1 = (f32[128,128]{1,0:T(8,128)}, f32[128,128]{1,0:T(8,128)S(1)}, u32[]{:S(2)}) copy-start(f32[128,128]{1,0:T(8,128)S(1)} %get-tuple-element.54) | copy-start | bytes 196612
  33.5 0.6 %copy-start.6 = (s32[128,128]{1,0:T(8,128)}, s32[128,128]{1,0:T(8,128)S(1)}, u32[]{:S(2)}) copy-start(s32[128,128]{1,0:T(8,128)S(1)} %get-tuple-element.55) | copy-start | bytes 196612

commit v2 on v1

--- a/solution.py
+++ b/solution.py
@@ -17,6 +17,7 @@
 BLOCK = LANES * LANES
 CUT = 15
 LOW = (1 << CUT) - 1
+PITCH = ROWS + 1
 
 
 def sub_iota():
@@ -43,8 +44,8 @@
     return ("s", bit) if bit < 3 else ("v", bit - 3) if bit < 7 else ("l", bit - 7)
 
 
-def flip(regs, bit, linear):
-    kind, at = place(bit, linear)
+def flip(regs, spot):
+    kind, at = spot
     if kind == "v":
         return [~x if g >> at & 1 else x for g, x in enumerate(regs)]
     index = sub_iota() if kind == "s" else lane_iota()
@@ -52,47 +53,55 @@
     return [x ^ mask for x in regs]
 
 
-def exchange(keys, loads, bit, linear):
-    kind, at = place(bit, linear)
-    keys, loads = list(keys), list(loads)
-    if kind == "v":
-        for low in range(len(keys)):
-            high = low | 1 << at
-            if high == low:
-                continue
-            a, b, p, q = keys[low], keys[high], loads[low], loads[high]
-            swap = a > b
-            keys[low], keys[high] = jnp.minimum(a, b), jnp.maximum(a, b)
-            loads[low], loads[high] = jnp.where(swap, q, p), jnp.where(swap, p, q)
-        return keys, loads
-    step = 1 << at
-    upper = (sub_iota() >> at & 1) == 1
-
-    def partner(x):
-        if 2 * step == ROWS:
-            return pltpu.roll(x, step, 0)
-        return jnp.where(upper, pltpu.roll(x, step, 0), pltpu.roll(x, ROWS - step, 0))
-
-    for g, (a, p) in enumerate(zip(keys, loads)):
-        b, q = partner(a), partner(p)
-        new = jnp.where(upper, jnp.maximum(a, b), jnp.minimum(a, b))
-        keys[g], loads[g] = new, jnp.where(new == a, p, q)
-    return keys, loads
-
-
-def sort_pairs(keys, loads, first_level, linear):
-    bits = (len(keys) * TILE).bit_length() - 1
-    for level in range(first_level, bits + 1):
-        if level > first_level:
-            keys = flip(keys, level - 1, linear)
+def swapped(regs, ref):
+    for g, x in enumerate(regs):
+        ref[pl.ds(PITCH * g, ROWS), :] = x
+    return [
+        ref[pl.ds(PITCH * (g & ~7) + (g & 7), ROWS, stride=PITCH), :] for g in range(len(regs))
+    ]
+
+
+def sort_levels(keys, loads, spots, levels, key_ref, load_ref):
+    bits = len(spots)
+
+    def moved(pairs, change):
+        names = dict(pairs) | {b: a for a, b in pairs}
+        spots[:] = [names.get(spot, spot) for spot in spots]
+        keys[:], loads[:] = change(keys, key_ref), change(loads, load_ref)
+
+    def turn():
+        pairs = [(("s", b), ("l", b)) for b in range(3)]
+        pairs += [(("v", b), ("l", b + 3)) for b in range(4)]
+        moved(pairs, lambda regs, ref: turned(regs))
+
+    def swap():
+        moved([(("s", b), ("v", b)) for b in range(3)], swapped)
+
+    for level in levels:
+        if level > levels[0]:
+            keys[:] = flip(keys, spots[level - 1])
         if level < bits:
-            keys = flip(keys, level, linear)
+            keys[:] = flip(keys, spots[level])
         for bit in reversed(range(level)):
-            if bit < 14 and linear != (bit >= 7):
-                keys, loads, linear = turned(keys), turned(loads), not linear
-            keys, loads = exchange(keys, loads, bit, linear)
-    assert not linear
-    return keys, loads
+            if spots[bit][0] == "l":
+                if level == bits and bit < 7 and spots[7][0] == "v":
+                    swap()
+                turn()
+            if spots[bit][0] == "s":
+                swap()
+            at = spots[bit][1]
+            for low in range(len(keys)):
+                high = low | 1 << at
+                if high == low:
+                    continue
+                a, b, p, q = keys[low], keys[high], loads[low], loads[high]
+                larger = a > b
+                keys[low], keys[high] = jnp.minimum(a, b), jnp.maximum(a, b)
+                loads[low], loads[high] = jnp.where(larger, q, p), jnp.where(larger, p, q)
+    if levels[-1] < bits:
+        keys[:] = flip(keys, spots[levels[-1]])
+    elif spots[0][0] == "v":
+        swap()
 
 
 def lane_next(regs, fill):
@@ -250,10 +259,12 @@
     new_move, new_load = shift(move, bit, linear), shift(load, bit, linear)
     for g in range(len(move)):
         arrives = (new_move[g] & probe) != 0
-        leaves = (move[g] & probe) != 0
-        stay = load[g] if empty is None else jnp.where(leaves, empty, load[g])
-        new_move[g] = jnp.where(arrives, new_move[g], jnp.where(leaves, 0, move[g]))
-        new_load[g] = jnp.where(arrives, new_load[g], stay)
+        old_move, old_load = move[g], load[g]
+        if empty is not None:
+            leaves = (old_move & probe) != 0
+            old_move, old_load = jnp.where(leaves, 0, old_move), jnp.where(leaves, empty, old_load)
+        new_move[g] = jnp.where(arrives, new_move[g], old_move)
+        new_load[g] = jnp.where(arrives, new_load[g], old_load)
     return new_move, new_load
 
 
@@ -271,22 +282,66 @@
     return [x & LOW for x in move], keys, total
 
 
-def split_kernel(own, slots, chunk, round_ref, odd_ref, cell_ref, vehicle_ref, speed_ref, out_ref, low_ref, high_ref):
+def owner_sizes(flags, cells, n, shift):
+    sums = [jnp.zeros((ROWS, LANES), jnp.int32)] * (n // 4)
+    for w, c in zip(flags, cells):
+        group = jnp.where(w, c >> (shift + 2), -1)
+        unit = jnp.left_shift(1, (c >> (shift - 3)) & 24)
+        sums = [x + jnp.where(group == k, unit, 0) for k, x in enumerate(sums)]
+    sizes = []
+    for x in sums:
+        pairs = []
+        for part in (x & 0xFF00FF, (x >> 8) & 0xFF00FF):
+            for step in (4, 2, 1):
+                part = part + pltpu.roll(part, step, 0)
+            pairs.append(part)
+        for half in (0, 16):
+            for part in pairs:
+                row = (part >> half) & 0xFFFF
+                sizes.append(jnp.sum(jnp.where(sub_iota() == 0, row, 0)))
+    return sizes
+
+
+def split_kernel(own, slots, chunk, round_ref, odd_ref, cell_in, vehicle_in, speed_in, out_hbm, cell_ref, vehicle_ref, speed_ref, out_ref, low_ref, high_ref, cell_pad, key_pad, in_sem, out_sem):
     n = CELLS // own
     count = cell_ref.shape[0] // ROWS
+    bits = (count * TILE).bit_length() - 1
     odd = odd_ref[0]
+    arrays = ((cell_in, cell_ref), (vehicle_in, vehicle_ref), (speed_in, speed_ref))
+    copies = []
+    for h in range(count // 16):
+        part = pl.ds(LANES * h, LANES)
+        copies.append(
+            [
+                pltpu.make_async_copy(x.at[part, :], y.at[part, :], in_sem.at[h, k])
+                for k, (x, y) in enumerate(arrays)
+            ]
+        )
+        for copy in copies[h]:
+            copy.start()
     cells, keys = [], []
-    for g in range(count):
-        at = pl.ds(ROWS * g, ROWS)
-        cell = cell_ref[at, :]
-        cells.append(jnp.where(odd == 1, CELLS - 1 - cell, cell))
-        level = (speed_ref[at, :] * float(STEPS)).astype(jnp.int32)
-        keys.append(level * VEHICLES + (VEHICLES - 1 - vehicle_ref[at, :]))
-    cells, keys = sort_pairs(cells, keys, 1, False)
+    for h in range(count // 16):
+        for copy in copies[h]:
+            copy.wait()
+        some_cells, some_keys = [], []
+        for g in range(16 * h, 16 * h + 16):
+            at = pl.ds(ROWS * g, ROWS)
+            cell = cell_ref[at, :]
+            some_cells.append(jnp.where(odd == 1, CELLS - 1 - cell, cell))
+            level = (speed_ref[at, :] * float(STEPS)).astype(jnp.int32)
+            some_keys.append(level * VEHICLES + (VEHICLES - 1 - vehicle_ref[at, :]))
+        spots = [place(bit, False) for bit in range(bits)]
+        pad = pl.ds(16 * PITCH * h, 16 * PITCH)
+        sort_levels(
+            some_cells, some_keys, spots, range(1, 8), cell_pad.at[pad, :], key_pad.at[pad, :]
+        )
+        cells += some_cells
+        keys += some_keys
+    sort_levels(cells, keys, spots, range(8, bits + 1), cell_pad, key_pad)
     keys = run_max(cells, keys)
     ends = run_ends(cells)
     shift = own.bit_length() - 1
-    owner = [jnp.where(w, c >> shift, -1) for w, c in zip(ends, cells)]
+    sizes = owner_sizes(ends, cells, n, shift)
     high = [k | (c >> CUT) << 27 for k, c in zip(keys, cells)]
     low, high, _ = compact([c & LOW for c in cells], high, ends)
     for g in range(count):
@@ -295,12 +350,20 @@
         high_ref[at, :] = high[g]
     low_ref[pl.ds(ROWS * count, ROWS), :] = jnp.zeros((ROWS, LANES), jnp.int32)
     high_ref[pl.ds(ROWS * count, ROWS), :] = jnp.zeros((ROWS, LANES), jnp.int32)
-    sizes = [jnp.sum(sum(jnp.where(w == o, 1, 0) for w in owner)) for o in range(n)]
     most = functools.reduce(jnp.maximum, sizes)
     sub, lane = sub_iota(), lane_iota()
     skip = round_ref[0] * (slots * LANES)
     base = jnp.int32(0)
+    group = n // 4
+    writes = []
+    for k in range(4):
+        part = pl.ds(jnp.where(odd == 1, 3 - k, k) * (group * chunk), group * chunk)
+        writes.append(
+            pltpu.make_async_copy(out_ref.at[part, :], out_hbm.at[part, :], out_sem.at[k])
+        )
     for o in range(n):
+        if o % group == 0 and o > group:
+            writes[o // group - 2].start()
         start = base + skip
         valid = sub * LANES + lane < sizes[o] - skip
         start = jnp.minimum(start, count * TILE)
@@ -313,22 +376,26 @@
 
         low_w, high_w = window(low_ref), window(high_ref)
         cell = jnp.where(valid, low_w & (own - 1), own).astype(jnp.float32)
-        key = jnp.where(valid, high_w & ((1 << 27) - 1), 0)
-        speed = (key >> 10).astype(jnp.float32) * (1.0 / STEPS)
-        ident = (VEHICLES - 1 - (key & (VEHICLES - 1))).astype(jnp.float32)
+        level = (high_w & ((1 << 27) - 1)) >> 10
+        speed = level.astype(jnp.float32) * (1.0 / STEPS)
+        ident = (~high_w & (VEHICLES - 1)).astype(jnp.float32)
         target = pl.multiple_of(jnp.where(odd == 1, n - 1 - o, o) * chunk, chunk)
         for w, x in enumerate((cell, speed, ident)):
             out_ref[pl.ds(target + w * slots, slots), :] = x[:slots]
         tail = chunk - 3 * slots
         fill = jnp.full((tail, LANES), most.astype(jnp.float32))
         out_ref[pl.ds(target + 3 * slots, tail), :] = fill
-
-
-def join_kernel(own, n, slots, chunk, in_ref, speed_ref, ident_ref, most_ref):
+    for k in (2, 3):
+        writes[k].start()
+    for write in writes:
+        write.wait()
+
+
+def join_kernel(own, n, slots, chunk, in_ref, speed_ref, ident_ref, rounds_ref, cell_pad, key_pad):
     sub = sub_iota()
     per = ROWS // run_rows(slots)
     cells, keys = [], []
-    most = jnp.zeros((1, LANES), jnp.float32)
+    most = jnp.zeros((ROWS, LANES), jnp.float32)
     for g in range(n // per):
         if per == 1:
             part = [in_ref[pl.ds(chunk * g + w * slots, slots), :] for w in range(3)]
@@ -341,7 +408,7 @@
             live = sub >= 0
             source = sub & 1
         for k in range(per):
-            most = jnp.maximum(most, in_ref[pl.ds(chunk * (per * g + k + 1) - 1, 1), :])
+            most = jnp.maximum(most, in_ref[pl.ds(chunk * (per * g + k + 1) - ROWS, ROWS), :])
         cell = jnp.where(live, part[0].astype(jnp.int32), own)
         if per == 1:
             cell = own - 1 - cell if source else cell
@@ -350,9 +417,12 @@
         level = (part[1] * float(STEPS)).astype(jnp.int32)
         cells.append(cell)
         keys.append(level * VEHICLES + (VEHICLES - 1 - part[2].astype(jnp.int32)))
-    most_ref[...] = most
+    most = jnp.max(jnp.where(sub == ROWS - 1, most, 0.0)).astype(jnp.int32)
+    rounds_ref[0] = lax.div(most + (slots * LANES - 1), jnp.int32(slots * LANES))
     first = (run_rows(slots) * LANES).bit_length()
-    cells, keys = sort_pairs(cells, keys, first, True)
+    bits = (len(cells) * TILE).bit_length() - 1
+    spots = [place(bit, True) for bit in range(bits)]
+    sort_levels(cells, keys, spots, range(first, bits + 1), cell_pad, key_pad)
     keys = run_max(cells, keys)
     ends = [w & (c >= 0) & (c < own) for w, c in zip(run_ends(cells), cells)]
     cells, keys, total = compact(cells, keys, ends)
@@ -378,6 +448,10 @@
     return 1 << (slots - 1).bit_length()
 
 
+def pads(rows):
+    return [pltpu.VMEM((rows // ROWS * PITCH, LANES), jnp.int32)] * 2
+
+
 def per_device(cell, vehicle, speed):
     n = lax.axis_size(AXES)
     own = CELLS // n
@@ -387,6 +461,8 @@
     rows = events // LANES
     smem = pl.BlockSpec(memory_space=pltpu.SMEM)
     vmem = pl.BlockSpec(memory_space=pltpu.VMEM)
+    hbm = pl.BlockSpec(memory_space=pl.ANY)
+    params = pltpu.CompilerParams(vmem_limit_bytes=16 << 20)
     table = (own // LANES, LANES)
     odd = (lax.axis_index(AXES) & 1).reshape(1)
     inputs = [x.reshape(rows, LANES) for x in (cell, vehicle, speed)]
@@ -394,9 +470,19 @@
     split = pl.pallas_call(
         functools.partial(split_kernel, own, slots, chunk),
         out_shape=jax.ShapeDtypeStruct((n * chunk, LANES), jnp.float32),
-        in_specs=[smem, smem, vmem, vmem, vmem],
-        out_specs=vmem,
-        scratch_shapes=[pltpu.VMEM((rows + ROWS, LANES), jnp.int32)] * 2,
+        in_specs=[smem, smem, hbm, hbm, hbm],
+        out_specs=hbm,
+        scratch_shapes=[
+            pltpu.VMEM((rows, LANES), jnp.int32),
+            pltpu.VMEM((rows, LANES), jnp.int32),
+            pltpu.VMEM((rows, LANES), jnp.float32),
+            pltpu.VMEM((n * chunk, LANES), jnp.float32),
+            pltpu.VMEM((rows + ROWS, LANES), jnp.int32),
+            pltpu.VMEM((rows + ROWS, LANES), jnp.int32),
+        ]
+        + pads(rows)
+        + [pltpu.SemaphoreType.DMA((rows // LANES, 3)), pltpu.SemaphoreType.DMA((4,))],
+        compiler_params=params,
         name="split",
     )
     join = pl.pallas_call(
@@ -404,10 +490,12 @@
         out_shape=(
             jax.ShapeDtypeStruct(table, jnp.float32),
             jax.ShapeDtypeStruct(table, jnp.int32),
-            jax.ShapeDtypeStruct((1, LANES), jnp.float32),
+            jax.ShapeDtypeStruct((1,), jnp.int32),
         ),
         in_specs=[vmem],
-        out_specs=(vmem, vmem, vmem),
+        out_specs=(vmem, vmem, smem),
+        scratch_shapes=pads(n * run_rows(slots)),
+        compiler_params=params,
         name="join",
     )
 
@@ -416,8 +504,7 @@
         got = lax.all_to_all(sent.reshape(n, chunk, LANES), AXES, 0, 0, tiled=True)
         return join(got.reshape(n * chunk, LANES))
 
-    best, ident, most = one_round(jnp.int32(0))
-    rounds = -(-most[0, 0].astype(jnp.int32) // (slots * LANES))
+    best, ident, rounds = one_round(jnp.int32(0))
 
     def again(state):
         index, best, ident = state
@@ -428,7 +515,7 @@
         return index + 1, jnp.maximum(best, more), ident
 
     _, best, ident = lax.while_loop(
-        lambda state: state[0] < rounds, again, (jnp.int32(1), best, ident)
+        lambda state: state[0] < rounds[0], again, (jnp.int32(1), best, ident)
     )
     return best.reshape(own), ident.reshape(own)
 

time: 34.4 us -> 29.8 us (0.87)
  Pallas kernels: 13.6 us -> 9.7 us
  local copies, waits for them, and re-layouts: 2 us -> 0.65 us
  loops' own time: 0.19 us -> 0.86 us
    pallas_call x1, Pallas kernels: 5.41 us -> 3.32 us  [one_round(): return join(got.reshape(n * chunk, LANES))]
    pallas_call x1, Pallas kernels: 8.22 us -> 6.38 us  [one_round(): sent = split(index.reshape(1), odd, *inputs)]
    unnamed x14 -> x10, local copies, waits for them, and re-layouts: 2 us -> 0.65 us
    another operation x1, loops' own time: 0.19 us -> 0.86 us  [per_device(): lax.while_loop(lambda state: state[0] < rounds[0], again, (jnp.int32(1),...]
where the time goes in v2:
time: 29.8 us; the launch traced here: 29.5 us
  waiting for transfers between devices  10.3 us (35%)
  Pallas kernels  9.7 us (33%)
  starting transfers between devices  7.33 us (25%)
  loops' own time  0.86 us (3%)
  between operations  0.72 us (2%)
  local copies, waits for them, and re-layouts  0.65 us (2%)
    all_to_all x1, waiting for transfers between devices, one_round(): got = lax.all_to_all(sent.reshape(n, chunk, LANES), AXES, 0, 0, tiled=True)  10.3 us
    all_to_all x1, starting transfers between devices, one_round(): got = lax.all_to_all(sent.reshape(n, chunk, LANES), AXES, 0, 0, tiled=True)  7.33 us
    pallas_call x1, Pallas kernels, one_round(): sent = split(index.reshape(1), odd, *inputs)  6.38 us
    pallas_call x1, Pallas kernels, one_round(): return join(got.reshape(n * chunk, LANES))  3.32 us
    another operation x1, loops' own time, per_device(): lax.while_loop(lambda state: state[0] < rounds[0], again, (jnp.int32(1),...  0.86 us
    unnamed x10, local copies, waits for them, and re-layouts  0.65 us
  transfers between devices with their start and end apart: 1, of which 1 were waited for; matrix products, arithmetic and copies ran while one was open for 0% of the time, Pallas kernels for 0%

profile of v2, /device:TPU:0, one launch (start us, length us, event | category | flops | bytes accessed | tf_op | source)
XLA Modules:
  0.0 29.5 jit_solution(1089364608963908992)
XLA Ops:
  0.6 6.4 %split.2 = f32[512,128]{1,0:T(8,128)} custom-call(s32[1]{0:T(128)} %constant.5.clone.1.round_ref, s32[1]{0:T(128)} %bitcast.4.odd_ref, s32[256,128]{1,0:T(8,128)} %bitcast.22, s32[256,128]{1,0:T(8,128)} %bitcast.24, f32[256,128]{1,0:T(8,128)} %bitcast.26), custom_call_target="tpu_custom_call" | custom-call | tf_op jit(solution)/shard_map/split/pallas_call | solution.py:503
  7.0 0.0 copy-start.3
  7.0 7.3 %all-to-all-start.1 = ((f32[32,16,128]{2,1,0:T(8,128)}), f32[32,16,128]{2,1,0:T(8,128)S(1)}, u32[]{:S(2)}, u32[]{:S(2)}) async-start(f32[32,16,128]{2,1,0:T(8,128)} %bitcast.8), calls=%async_computation.1 | async-start | bytes 524288 | tf_op jit(solution)/shard_map/all_to_all | solution.py:504
  14.4 10.3 %all-to-all-done.1 = f32[32,16,128]{2,1,0:T(8,128)S(1)} async-done(((f32[32,16,128]{2,1,0:T(8,128)}), f32[32,16,128]{2,1,0:T(8,128)S(1)}, u32[]{:S(2)}, u32[]{:S(2)}) %all-to-all-start.1) | async-done | bytes 262176 | tf_op jit(solution)/shard_map/all_to_all | solution.py:504
  24.6 0.0 copy-start.1
  24.6 0.0 copy-start.2
  24.6 3.3 %join.2 = (f32[128,128]{1,0:T(8,128)S(1)}, s32[128,128]{1,0:T(8,128)S(1)}, s32[1]{0:T(128)}) custom-call(f32[512,128]{1,0:T(8,128)S(1)} %bitcast.20), custom_call_target="tpu_custom_call" | custom-call | tf_op jit(solution)/shard_map/join/pallas_call | solution.py:505
  28.0 0.0 copy-done.3
  28.0 0.0 copy-done.1
  28.0 0.0 copy-done.2
  28.0 0.9 %while.12 = (s32[]{:T(128)}, f32[128,128]{1,0:T(8,128)S(1)}, s32[128,128]{1,0:T(8,128)S(1)}, s32[1]{0:T(128)}, s32[1]{0:T(128)}, /*index=5*/s32[256,128]{1,0:T(8...) while((s32[]{:T(128)}, f32[128,128]{1,0:T(8,128)S(1)}, s32[128,128]{1,0:T(8,128)S(1)}, ...), condition=%wide.region_1.2_spmd, body=%wide.region_0.1_spmd.sunk | while | flops 98306 | bytes 1310845 | solution.py:517
  28.9 0.0 copy-start
  28.9 0.0 copy-start.4
  28.9 0.6 %copy-done = f32[128,128]{1,0:T(8,128)} copy-done((f32[128,128]{1,0:T(8,128)}, f32[128,128]{1,0:T(8,128)S(1)}, u32[]{:S(2)}) %copy-start) | copy-done | bytes 65560
  29.5 0.0 copy-done.4
Async XLA Ops:
  7.0 20.9 %copy-start.3 = (f32[32768]{0:T(1024)S(1)}, f32[32768]{0:T(1024)}, u32[]{:S(2)}) copy-start(f32[32768]{0:T(1024)} %param.7) | copy-start | bytes 393220
  7.0 17.6 %all-to-all-start.1 = ((f32[32,16,128]{2,1,0:T(8,128)}), f32[32,16,128]{2,1,0:T(8,128)S(1)}, u32[]{:S(2)}, u32[]{:S(2)}) async-start(f32[32,16,128]{2,1,0:T(8,128)} %bitcast.8), calls=%async_computation.1 | async-start | bytes 524288 | tf_op jit(solution)/shard_map/all_to_all | solution.py:504
  24.6 3.3 %copy-start.1 = (s32[32768]{0:T(1024)S(1)}, s32[32768]{0:T(1024)}, u32[]{:S(2)}) copy-start(s32[32768]{0:T(1024)} %param.5) | copy-start | bytes 393220
  24.6 3.4 %copy-start.2 = (s32[32768]{0:T(1024)S(1)}, s32[32768]{0:T(1024)}, u32[]{:S(2)}) copy-start(s32[32768]{0:T(1024)} %param.6) | copy-start | bytes 393220
  28.9 0.6 %copy-start = (f32[128,128]{1,0:T(8,128)}, f32[128,128]{1,0:T(8,128)S(1)}, u32[]{:S(2)}) copy-start(f32[128,128]{1,0:T(8,128)S(1)} %get-tuple-element.54) | copy-start | bytes 196612
  28.9 0.6 %copy-start.4 = (s32[128,128]{1,0:T(8,128)}, s32[128,128]{1,0:T(8,128)S(1)}, u32[]{:S(2)}) copy-start(s32[128,128]{1,0:T(8,128)S(1)} %get-tuple-element.55) | copy-start | bytes 196612

commit v3 on v2

--- a/solution.py
+++ b/solution.py
@@ -44,15 +44,6 @@
     return ("s", bit) if bit < 3 else ("v", bit - 3) if bit < 7 else ("l", bit - 7)
 
 
-def flip(regs, spot):
-    kind, at = spot
-    if kind == "v":
-        return [~x if g >> at & 1 else x for g, x in enumerate(regs)]
-    index = sub_iota() if kind == "s" else lane_iota()
-    mask = -((index >> at) & 1)
-    return [x ^ mask for x in regs]
-
-
 def swapped(regs, ref):
     for g, x in enumerate(regs):
         ref[pl.ds(PITCH * g, ROWS), :] = x
@@ -61,47 +52,100 @@
     ]
 
 
-def sort_levels(keys, loads, spots, levels, key_ref, load_ref):
-    bits = len(spots)
-
-    def moved(pairs, change):
+def exchange(keys, loads, low, high, more_keys=None, more_loads=None):
+    more_keys = keys if more_keys is None else more_keys
+    more_loads = loads if more_loads is None else more_loads
+    a, b, p, q = keys[low], more_keys[high], loads[low], more_loads[high]
+    larger = a > b
+    keys[low], more_keys[high] = jnp.minimum(a, b), jnp.maximum(a, b)
+    loads[low], more_loads[high] = jnp.where(larger, q, p), jnp.where(larger, p, q)
+
+
+class Block:
+    def __init__(self, load, index, linear, key_ref, load_ref):
+        self.load, self.index = load, index
+        self.spots = [place(bit, linear) for bit in range(14)]
+        at = pl.ds(16 * PITCH * index, 16 * PITCH)
+        self.refs = key_ref.at[at, :], load_ref.at[at, :]
+        self.faced = None
+
+    def moved(self, pairs, change):
         names = dict(pairs) | {b: a for a, b in pairs}
-        spots[:] = [names.get(spot, spot) for spot in spots]
-        keys[:], loads[:] = change(keys, key_ref), change(loads, load_ref)
-
-    def turn():
+        self.spots = [names.get(spot, spot) for spot in self.spots]
+        self.keys = change(self.keys, self.refs[0])
+        self.loads = change(self.loads, self.refs[1])
+
+    def turn(self):
         pairs = [(("s", b), ("l", b)) for b in range(3)]
         pairs += [(("v", b), ("l", b + 3)) for b in range(4)]
-        moved(pairs, lambda regs, ref: turned(regs))
-
-    def swap():
-        moved([(("s", b), ("v", b)) for b in range(3)], swapped)
-
-    for level in levels:
-        if level > levels[0]:
-            keys[:] = flip(keys, spots[level - 1])
-        if level < bits:
-            keys[:] = flip(keys, spots[level])
-        for bit in reversed(range(level)):
-            if spots[bit][0] == "l":
-                if level == bits and bit < 7 and spots[7][0] == "v":
-                    swap()
-                turn()
-            if spots[bit][0] == "s":
-                swap()
-            at = spots[bit][1]
-            for low in range(len(keys)):
-                high = low | 1 << at
-                if high == low:
-                    continue
-                a, b, p, q = keys[low], keys[high], loads[low], loads[high]
-                larger = a > b
-                keys[low], keys[high] = jnp.minimum(a, b), jnp.maximum(a, b)
-                loads[low], loads[high] = jnp.where(larger, q, p), jnp.where(larger, p, q)
-    if levels[-1] < bits:
-        keys[:] = flip(keys, spots[levels[-1]])
-    elif spots[0][0] == "v":
-        swap()
+        self.moved(pairs, lambda regs, ref: turned(regs))
+
+    def swap(self):
+        self.moved([(("s", b), ("v", b)) for b in range(3)], swapped)
+
+    def face(self, bit):
+        odd, mask = [0] * 16, None
+        for each in {self.faced, bit} - {None}:
+            kind, at = self.spots[each] if each < 14 else ("h", each - 14)
+            if kind == "h":
+                odd = [x ^ (self.index >> at & 1) for x in odd]
+            elif kind == "v":
+                odd = [x ^ (g >> at & 1) for g, x in enumerate(odd)]
+            else:
+                index = sub_iota() if kind == "s" else lane_iota()
+                one = -((index >> at) & 1)
+                mask = one if mask is None else mask ^ one
+        if mask is None:
+            self.keys = [~x if o else x for x, o in zip(self.keys, odd)]
+        else:
+            masks = mask, ~mask
+            self.keys = [x ^ masks[o] for x, o in zip(self.keys, odd)]
+        self.faced = bit
+
+    def levels(self, levels, bits):
+        if self.load is not None:
+            self.keys, self.loads = self.load()
+            self.load = None
+        for level in levels:
+            if level < 15:
+                self.face(level if level < bits else None)
+            for bit in reversed(range(min(level, 14))):
+                if self.spots[bit][0] == "l":
+                    if level == bits and bit < 7 and self.spots[7][0] == "v":
+                        self.swap()
+                    yield
+                    self.turn()
+                if self.spots[bit][0] == "s":
+                    self.swap()
+                at = 1 << self.spots[bit][1]
+                for low in range(16):
+                    if not low & at:
+                        exchange(self.keys, self.loads, low, low | at)
+            if level == bits and self.spots[0][0] == "v":
+                self.swap()
+
+
+def run_all(takes):
+    takes = list(takes)
+    while takes:
+        takes = [take for take in takes if next(take, takes) is not takes]
+
+
+def sort_blocks(blocks, first):
+    bits = 13 + len(blocks).bit_length()
+    run_all(block.levels(range(first, min(bits, 14) + 1), bits) for block in blocks)
+    for level in range(15, bits + 1):
+        for block in blocks:
+            block.face(level if level < bits else None)
+        for bit in reversed(range(14, level)):
+            for one in blocks:
+                other = blocks[one.index | 1 << (bit - 14)]
+                if other is not one:
+                    for g in range(16):
+                        exchange(one.keys, one.loads, g, g, other.keys, other.loads)
+        run_all(block.levels([level], bits) for block in blocks)
+    keys = sum((block.keys for block in blocks), [])
+    return keys, sum((block.loads for block in blocks), [])
 
 
 def lane_next(regs, fill):
@@ -319,7 +363,7 @@
         )
         for copy in copies[h]:
             copy.start()
-    cells, keys = [], []
+    blocks = []
     for h in range(count // 16):
         for copy in copies[h]:
             copy.wait()
@@ -330,14 +374,10 @@
             some_cells.append(jnp.where(odd == 1, CELLS - 1 - cell, cell))
             level = (speed_ref[at, :] * float(STEPS)).astype(jnp.int32)
             some_keys.append(level * VEHICLES + (VEHICLES - 1 - vehicle_ref[at, :]))
-        spots = [place(bit, False) for bit in range(bits)]
-        pad = pl.ds(16 * PITCH * h, 16 * PITCH)
-        sort_levels(
-            some_cells, some_keys, spots, range(1, 8), cell_pad.at[pad, :], key_pad.at[pad, :]
-        )
-        cells += some_cells
-        keys += some_keys
-    sort_levels(cells, keys, spots, range(8, bits + 1), cell_pad, key_pad)
+        block = Block(lambda: (some_cells, some_keys), h, False, cell_pad, key_pad)
+        run_all([block.levels(range(1, 8), bits)])
+        blocks.append(block)
+    cells, keys = sort_blocks(blocks, 8)
     keys = run_max(cells, keys)
     ends = run_ends(cells)
     shift = own.bit_length() - 1
@@ -394,35 +434,38 @@
 def join_kernel(own, n, slots, chunk, in_ref, speed_ref, ident_ref, rounds_ref, cell_pad, key_pad):
     sub = sub_iota()
     per = ROWS // run_rows(slots)
-    cells, keys = [], []
+
+    def load(h):
+        cells, keys = [], []
+        late = jnp.where(blocks[h - 1].loads[15] > 1 << 30, 1, 0) if h else 0
+        for g in range(16 * h, 16 * h + 16):
+            if per == 1:
+                part = [in_ref[pl.ds(chunk * g + w * slots, slots), :] for w in range(3)]
+                pad = jnp.zeros((ROWS - slots, LANES), jnp.float32)
+                part = [jnp.concatenate([x, pad], axis=0) for x in part]
+                cell = jnp.where(sub < slots, part[0].astype(jnp.int32), own)
+                cell = own - 1 - cell if g & 1 else cell
+            else:
+                part = [
+                    in_ref[pl.ds(chunk * per * g + w, ROWS, stride=chunk), :] for w in range(3)
+                ]
+                cell = part[0].astype(jnp.int32)
+                cell = jnp.where(sub & 1 == 1, own - 1 - cell, cell)
+            level = (part[1] * float(STEPS)).astype(jnp.int32)
+            cells.append(cell + late)
+            keys.append(level * VEHICLES + (VEHICLES - 1 - part[2].astype(jnp.int32)))
+        return cells, keys
+
     most = jnp.zeros((ROWS, LANES), jnp.float32)
-    for g in range(n // per):
-        if per == 1:
-            part = [in_ref[pl.ds(chunk * g + w * slots, slots), :] for w in range(3)]
-            pad = jnp.zeros((ROWS - slots, LANES), jnp.float32)
-            part = [jnp.concatenate([x, pad], axis=0) for x in part]
-            live = sub < slots
-            source = g & 1
-        else:
-            part = [in_ref[pl.ds(chunk * per * g + w, ROWS, stride=chunk), :] for w in range(3)]
-            live = sub >= 0
-            source = sub & 1
-        for k in range(per):
-            most = jnp.maximum(most, in_ref[pl.ds(chunk * (per * g + k + 1) - ROWS, ROWS), :])
-        cell = jnp.where(live, part[0].astype(jnp.int32), own)
-        if per == 1:
-            cell = own - 1 - cell if source else cell
-        else:
-            cell = jnp.where(source == 1, own - 1 - cell, cell)
-        level = (part[1] * float(STEPS)).astype(jnp.int32)
-        cells.append(cell)
-        keys.append(level * VEHICLES + (VEHICLES - 1 - part[2].astype(jnp.int32)))
+    for source in range(n):
+        most = jnp.maximum(most, in_ref[pl.ds(chunk * (source + 1) - ROWS, ROWS), :])
     most = jnp.max(jnp.where(sub == ROWS - 1, most, 0.0)).astype(jnp.int32)
     rounds_ref[0] = lax.div(most + (slots * LANES - 1), jnp.int32(slots * LANES))
     first = (run_rows(slots) * LANES).bit_length()
-    bits = (len(cells) * TILE).bit_length() - 1
-    spots = [place(bit, True) for bit in range(bits)]
-    sort_levels(cells, keys, spots, range(first, bits + 1), cell_pad, key_pad)
+    blocks = [
+        Block(functools.partial(load, h), h, True, cell_pad, key_pad) for h in range(n // per // 16)
+    ]
+    cells, keys = sort_blocks(blocks, first)
     keys = run_max(cells, keys)
     ends = [w & (c >= 0) & (c < own) for w, c in zip(run_ends(cells), cells)]
     cells, keys, total = compact(cells, keys, ends)

time: 29.8 us -> 29.1 us (0.977)
  Pallas kernels: 9.7 us -> 9 us
    pallas_call x1, Pallas kernels: 6.38 us -> 5.77 us  [one_round(): sent = split(index.reshape(1), odd, *inputs)]
where the time goes in v3:
time: 29.1 us; the launch traced here: 28.8 us
  waiting for transfers between devices  10.3 us (35%)
  Pallas kernels  9 us (31%)
  starting transfers between devices  7.33 us (25%)
  loops' own time  0.86 us (3%)
  between operations  0.72 us (2%)
  local copies, waits for them, and re-layouts  0.65 us (2%)
    all_to_all x1, waiting for transfers between devices, one_round(): got = lax.all_to_all(sent.reshape(n, chunk, LANES), AXES, 0, 0, tiled=True)  10.3 us
    all_to_all x1, starting transfers between devices, one_round(): got = lax.all_to_all(sent.reshape(n, chunk, LANES), AXES, 0, 0, tiled=True)  7.33 us
    pallas_call x1, Pallas kernels, one_round(): sent = split(index.reshape(1), odd, *inputs)  5.77 us
    pallas_call x1, Pallas kernels, one_round(): return join(got.reshape(n * chunk, LANES))  3.24 us
    another operation x1, loops' own time, per_device(): lax.while_loop(lambda state: state[0] < rounds[0], again, (jnp.int32(1),...  0.86 us
    unnamed x10, local copies, waits for them, and re-layouts  0.65 us
  transfers between devices with their start and end apart: 1, of which 1 were waited for; matrix products, arithmetic and copies ran while one was open for 0% of the time, Pallas kernels for 0%

profile of v3, /device:TPU:0, one launch (start us, length us, event | category | flops | bytes accessed | tf_op | source)
XLA Modules:
  0.0 28.8 jit_solution(8460978519911804256)
XLA Ops:
  0.6 5.8 %split.2 = f32[512,128]{1,0:T(8,128)} custom-call(s32[1]{0:T(128)} %constant.5.clone.1.round_ref, s32[1]{0:T(128)} %bitcast.4.odd_ref, s32[256,128]{1,0:T(8,128)} %bitcast.22, s32[256,128]{1,0:T(8,128)} %bitcast.24, f32[256,128]{1,0:T(8,128)} %bitcast.26), custom_call_target="tpu_custom_call" | custom-call | tf_op jit(solution)/shard_map/split/pallas_call | solution.py:546
  6.4 0.0 copy-start.3
  6.4 7.3 %all-to-all-start.1 = ((f32[32,16,128]{2,1,0:T(8,128)}), f32[32,16,128]{2,1,0:T(8,128)S(1)}, u32[]{:S(2)}, u32[]{:S(2)}) async-start(f32[32,16,128]{2,1,0:T(8,128)} %bitcast.8), calls=%async_computation.1 | async-start | bytes 524288 | tf_op jit(solution)/shard_map/all_to_all | solution.py:547
  13.8 10.3 %all-to-all-done.1 = f32[32,16,128]{2,1,0:T(8,128)S(1)} async-done(((f32[32,16,128]{2,1,0:T(8,128)}), f32[32,16,128]{2,1,0:T(8,128)S(1)}, u32[]{:S(2)}, u32[]{:S(2)}) %all-to-all-start.1) | async-done | bytes 262176 | tf_op jit(solution)/shard_map/all_to_all | solution.py:547
  24.0 0.0 copy-start.1
  24.0 0.0 copy-start.2
  24.0 3.2 %join.2 = (f32[128,128]{1,0:T(8,128)S(1)}, s32[128,128]{1,0:T(8,128)S(1)}, s32[1]{0:T(128)}) custom-call(f32[512,128]{1,0:T(8,128)S(1)} %bitcast.20), custom_call_target="tpu_custom_call" | custom-call | tf_op jit(solution)/shard_map/join/pallas_call | solution.py:548
  27.3 0.0 copy-done.3
  27.3 0.0 copy-done.1
  27.3 0.0 copy-done.2
  27.3 0.9 %while.12 = (s32[]{:T(128)}, f32[128,128]{1,0:T(8,128)S(1)}, s32[128,128]{1,0:T(8,128)S(1)}, s32[1]{0:T(128)}, s32[1]{0:T(128)}, /*index=5*/s32[256,128]{1,0:T(8...) while((s32[]{:T(128)}, f32[128,128]{1,0:T(8,128)S(1)}, s32[128,128]{1,0:T(8,128)S(1)}, ...), condition=%wide.region_1.2_spmd, body=%wide.region_0.1_spmd.sunk | while | flops 98306 | bytes 1310845 | solution.py:560
  28.2 0.0 copy-start
  28.2 0.0 copy-start.4
  28.2 0.6 %copy-done = f32[128,128]{1,0:T(8,128)} copy-done((f32[128,128]{1,0:T(8,128)}, f32[128,128]{1,0:T(8,128)S(1)}, u32[]{:S(2)}) %copy-start) | copy-done | bytes 65560
  28.8 0.0 copy-done.4
Async XLA Ops:
  6.4 20.9 %copy-start.3 = (f32[32768]{0:T(1024)S(1)}, f32[32768]{0:T(1024)}, u32[]{:S(2)}) copy-start(f32[32768]{0:T(1024)} %param.7) | copy-start | bytes 393220
  6.4 17.6 %all-to-all-start.1 = ((f32[32,16,128]{2,1,0:T(8,128)}), f32[32,16,128]{2,1,0:T(8,128)S(1)}, u32[]{:S(2)}, u32[]{:S(2)}) async-start(f32[32,16,128]{2,1,0:T(8,128)} %bitcast.8), calls=%async_computation.1 | async-start | bytes 524288 | tf_op jit(solution)/shard_map/all_to_all | solution.py:547
  24.0 3.3 %copy-start.1 = (s32[32768]{0:T(1024)S(1)}, s32[32768]{0:T(1024)}, u32[]{:S(2)}) copy-start(s32[32768]{0:T(1024)} %param.5) | copy-start | bytes 393220
  24.0 3.3 %copy-start.2 = (s32[32768]{0:T(1024)S(1)}, s32[32768]{0:T(1024)}, u32[]{:S(2)}) copy-start(s32[32768]{0:T(1024)} %param.6) | copy-start | bytes 393220
  28.2 0.6 %copy-start = (f32[128,128]{1,0:T(8,128)}, f32[128,128]{1,0:T(8,128)S(1)}, u32[]{:S(2)}) copy-start(f32[128,128]{1,0:T(8,128)S(1)} %get-tuple-element.54) | copy-start | bytes 196612
  28.2 0.6 %copy-start.4 = (s32[128,128]{1,0:T(8,128)}, s32[128,128]{1,0:T(8,128)S(1)}, u32[]{:S(2)}) copy-start(s32[128,128]{1,0:T(8,128)S(1)} %get-tuple-element.55) | copy-start | bytes 196612

commit v4 on v3

--- a/solution.py
+++ b/solution.py
@@ -121,8 +121,6 @@
                 for low in range(16):
                     if not low & at:
                         exchange(self.keys, self.loads, low, low | at)
-            if level == bits and self.spots[0][0] == "v":
-                self.swap()
 
 
 def run_all(takes):
@@ -185,6 +183,18 @@
     return out
 
 
+def pull_woven(regs, bit, linear):
+    step = 1 << bit
+    out = list(regs[step:]) + [None] * step
+    bottom = sub_iota() == ROWS - 1
+    for v in range(8 - step, 8):
+        rolled = [pltpu.roll(x, ROWS - 1, 0) for x in regs[v + step - 8 :: 8]]
+        wrap = lane_next(rolled[0::2], 0)
+        for c, x in enumerate(rolled):
+            out[8 * c + v] = jnp.where(bottom, wrap[c // 2] if c & 1 else rolled[c + 1], x)
+    return out
+
+
 def push(regs, bit, linear):
     assert len(regs) == 16
     kind, at = place(bit, linear)
@@ -224,22 +234,34 @@
 def run_max(cells, keys):
     count = len(cells)
     blocks = count // 16
-    sub = sub_iota()
+    sub, lane = sub_iota(), lane_iota()
     keys = list(keys)
+
+    def carry(g, cell, key, also=None):
+        same = cells[g] == cell
+        same = same if also is None else same & also
+        keys[g] = jnp.where(same, jnp.maximum(keys[g], key), keys[g])
+
+    for g in range(count):
+        if g % 8:
+            carry(g, cells[g - 1], keys[g - 1])
+    ends = range(7, count, 8)
+    final = [keys[g] for g in ends]
+    last = [cells[g] for g in ends]
+
+    def join(c, cell, key, also=None):
+        same = last[c] == cell
+        same = same if also is None else same & also
+        final[c] = jnp.where(same, jnp.maximum(final[c], key), final[c])
+
     for step in (1, 2, 4):
-        inside = sub >= step
-        for g in range(count):
-            same = (pltpu.roll(cells[g], step, 0) == cells[g]) & inside
-            keys[g] = jnp.where(same, jnp.maximum(keys[g], pltpu.roll(keys[g], step, 0)), keys[g])
-    for h in range(blocks):
-        for v in range(1, 16):
-            g = 16 * h + v
-            cell, key = spread_row(cells[g - 1], 7), spread_row(keys[g - 1], 7)
-            keys[g] = jnp.where(cells[g] == cell, jnp.maximum(keys[g], key), keys[g])
-    last_cell = [spread_row(cells[16 * h + 15], 7) for h in range(blocks)]
-    last_key = [spread_row(keys[16 * h + 15], 7) for h in range(blocks)]
+        for c in range(len(last)):
+            join(c, pltpu.roll(last[c], step, 0), pltpu.roll(final[c], step, 0), sub >= step)
+    for c in range(1, len(last), 2):
+        join(c, spread_row(last[c - 1], 7), spread_row(final[c - 1], 7))
+    last_cell = [spread_row(x, 7) for x in last[1::2]]
+    last_key = [spread_row(x, 7) for x in final[1::2]]
     rolled = [jnp.full((ROWS, LANES), -9, jnp.int32)] + [pltpu.roll(x, 1, 1) for x in last_cell]
-    lane = lane_iota()
     before = [jnp.where(lane == 0, rolled[h], rolled[h + 1]) for h in range(blocks)]
     cell_col = [down_lanes(x) for x in last_cell]
     key_col = [down_lanes(x) for x in last_key]
@@ -250,44 +272,61 @@
                 match = cell_col[source][v] == before[h]
                 if source == h:
                     match = match & (sub + ROWS * v < lane)
-                terms.append((match, key_col[source][v]))
-        terms = [jnp.where(match, key, -1) for match, key in terms]
-        while len(terms) % 16 or len(terms) & (len(terms) - 1):
+                terms.append(jnp.where(match, key_col[source][v], -1))
+        while len(terms) & (len(terms) - 1):
             terms.append(terms[0])
         best = over_rows(terms, jnp.maximum)
-        for g in range(16 * h, 16 * h + 16):
-            keys[g] = jnp.where(cells[g] == before[h], jnp.maximum(keys[g], best), keys[g])
+        for c in (2 * h, 2 * h + 1):
+            join(c, before[h], best)
+            cell, key = before[h], best
+            if c & 1:
+                cell, key = spread_row(last[c - 1], 7), spread_row(final[c - 1], 7)
+            cell = jnp.where(sub == 0, cell, pltpu.roll(last[c], 1, 0))
+            key = jnp.where(sub == 0, key, pltpu.roll(final[c], 1, 0))
+            for g in range(8 * c, 8 * c + 8):
+                carry(g, cell, key)
     return keys
 
 
 def run_ends(cells):
     count = len(cells)
-    rolled = [pltpu.roll(x, ROWS - 1, 0) for x in cells]
-    wrap = lane_next([rolled[16 * h] for h in range(count // 16)], -9)
-    over = [rolled[g + 1] if (g + 1) % 16 else wrap[g // 16] for g in range(count)]
     bottom = sub_iota() == ROWS - 1
-    return [c != jnp.where(bottom, b, a) for c, a, b in zip(cells, rolled, over)]
+    rolled = [pltpu.roll(x, ROWS - 1, 0) for x in cells[::8]]
+    wrap = lane_next(rolled[::2], -9)
+    out = []
+    for g in range(count):
+        c = g // 8
+        if g % 8 < 7:
+            after = cells[g + 1]
+        else:
+            after = jnp.where(bottom, wrap[c // 2] if c & 1 else rolled[c + 1], rolled[c])
+        out.append(cells[g] != after)
+    return out
 
 
 def ranks(flags):
     count = len(flags)
-    blocks = count // 16
     sub, lane = sub_iota(), lane_iota()
     out, total = [], jnp.zeros((ROWS, LANES), jnp.int32)
-    for h in range(blocks):
-        sums, run = [], jnp.zeros((ROWS, LANES), jnp.int32)
-        for v in range(16):
-            flag = flags[16 * h + v]
-            x = flag
+    for h in range(count // 16):
+        starts, run = [], jnp.zeros((ROWS, LANES), jnp.int32)
+        for c in (2 * h, 2 * h + 1):
+            here = jnp.zeros((ROWS, LANES), jnp.int32)
+            for g in range(8 * c, 8 * c + 8):
+                out.append(here)
+                here = here + flags[g]
+            x = here
             for step in (1, 2, 4):
                 x = x + jnp.where(sub >= step, pltpu.roll(x, step, 0), 0)
-            sums.append(x - flag + run)
+            starts.append(x - here + run)
             run = run + spread_row(x, 7)
         col = down_lanes(run)
         start = [jnp.where(sub + ROWS * v < lane, col[v], 0) for v in range(16)]
         start = over_rows(start, jnp.add) + total
         total = total + over_rows(col, jnp.add)
-        out += [x + start for x in sums]
+        starts = [x + start for x in starts]
+        for g in range(16 * h, 16 * h + 16):
+            out[g] = out[g] + starts[g // 8 % 2]
     return out, total
 
 
@@ -295,7 +334,8 @@
     sub, lane = sub_iota(), lane_iota()
     if linear:
         return [TILE * g + LANES * sub + lane for g in range(count)]
-    return [BLOCK * (g // 16) + LANES * lane + ROWS * (g % 16) + sub for g in range(count)]
+    weave = LANES * lane + ROWS * sub
+    return [weave + (BLOCK * (g // 16) + 64 * (g // 8 % 2) + g % 8) for g in range(count)]
 
 
 def travel(move, load, bit, linear, shift, empty):
@@ -312,7 +352,7 @@
     return new_move, new_load
 
 
-def compact(cells, keys, wanted):
+def compact(cells, keys, wanted, cell_ref, key_ref):
     count = len(cells)
     rank, total = ranks([jnp.where(w, 1, 0) for w in wanted])
     at = positions(count, False)
@@ -320,9 +360,11 @@
         jnp.where(w, (i - r) << CUT | c, 0) for w, i, r, c in zip(wanted, at, rank, cells)
     ]
     for bit in range((count * TILE).bit_length() - 1):
+        if bit == 3:
+            move, keys = swapped(move, cell_ref), swapped(keys, key_ref)
         if bit == 7:
             move, keys = turned(move), turned(keys)
-        move, keys = travel(move, keys, bit, bit >= 7, pull, None)
+        move, keys = travel(move, keys, bit, bit >= 7, pull if bit >= 3 else pull_woven, None)
     return [x & LOW for x in move], keys, total
 
 
@@ -383,7 +425,7 @@
     shift = own.bit_length() - 1
     sizes = owner_sizes(ends, cells, n, shift)
     high = [k | (c >> CUT) << 27 for k, c in zip(keys, cells)]
-    low, high, _ = compact([c & LOW for c in cells], high, ends)
+    low, high, _ = compact([c & LOW for c in cells], high, ends, cell_pad, key_pad)
     for g in range(count):
         at = pl.ds(ROWS * g, ROWS)
         low_ref[at, :] = low[g]
@@ -468,7 +510,7 @@
     cells, keys = sort_blocks(blocks, first)
     keys = run_max(cells, keys)
     ends = [w & (c >= 0) & (c < own) for w, c in zip(run_ends(cells), cells)]
-    cells, keys, total = compact(cells, keys, ends)
+    cells, keys, total = compact(cells, keys, ends, cell_pad, key_pad)
     keep = max(own // TILE, 1)
     at = positions(16, True)
     move = [jnp.where(i < total, (c - i) << CUT, 0) for i, c in zip(at, cells)]

time: 29.1 us -> 28.6 us (0.983)
  Pallas kernels: 9 us -> 8.54 us
where the time goes in v4:
time: 28.6 us; the launch traced here: 28.4 us
  waiting for transfers between devices  10.3 us (36%)
  Pallas kernels  8.54 us (30%)
  starting transfers between devices  7.33 us (26%)
  loops' own time  0.86 us (3%)
  between operations  0.72 us (3%)
  local copies, waits for them, and re-layouts  0.65 us (2%)
    all_to_all x1, waiting for transfers between devices, one_round(): got = lax.all_to_all(sent.reshape(n, chunk, LANES), AXES, 0, 0, tiled=True)  10.3 us
    all_to_all x1, starting transfers between devices, one_round(): got = lax.all_to_all(sent.reshape(n, chunk, LANES), AXES, 0, 0, tiled=True)  7.33 us
    pallas_call x1, Pallas kernels, one_round(): sent = split(index.reshape(1), odd, *inputs)  5.58 us
    pallas_call x1, Pallas kernels, one_round(): return join(got.reshape(n * chunk, LANES))  2.96 us
    another operation x1, loops' own time, per_device(): lax.while_loop(lambda state: state[0] < rounds[0], again, (jnp.int32(1),...  0.86 us
    unnamed x10, local copies, waits for them, and re-layouts  0.65 us
  transfers between devices with their start and end apart: 1, of which 1 were waited for; matrix products, arithmetic and copies ran while one was open for 0% of the time, Pallas kernels for 0%

profile of v4, /device:TPU:0, one launch (start us, length us, event | category | flops | bytes accessed | tf_op | source)
XLA Modules:
  0.0 28.4 jit_solution(14210463518123688457)
XLA Ops:
  0.6 5.6 %split.2 = f32[512,128]{1,0:T(8,128)} custom-call(s32[1]{0:T(128)} %constant.5.clone.1.round_ref, s32[1]{0:T(128)} %bitcast.4.odd_ref, s32[256,128]{1,0:T(8,128)} %bitcast.22, s32[256,128]{1,0:T(8,128)} %bitcast.24, f32[256,128]{1,0:T(8,128)} %bitcast.26), custom_call_target="tpu_custom_call" | custom-call | tf_op jit(solution)/shard_map/split/pallas_call | solution.py:588
  6.2 0.0 copy-start.3
  6.2 7.3 %all-to-all-start.1 = ((f32[32,16,128]{2,1,0:T(8,128)}), f32[32,16,128]{2,1,0:T(8,128)S(1)}, u32[]{:S(2)}, u32[]{:S(2)}) async-start(f32[32,16,128]{2,1,0:T(8,128)} %bitcast.8), calls=%async_computation.1 | async-start | bytes 524288 | tf_op jit(solution)/shard_map/all_to_all | solution.py:589
  13.6 10.3 %all-to-all-done.1 = f32[32,16,128]{2,1,0:T(8,128)S(1)} async-done(((f32[32,16,128]{2,1,0:T(8,128)}), f32[32,16,128]{2,1,0:T(8,128)S(1)}, u32[]{:S(2)}, u32[]{:S(2)}) %all-to-all-start.1) | async-done | bytes 262176 | tf_op jit(solution)/shard_map/all_to_all | solution.py:589
  23.8 0.0 copy-start.1
  23.8 0.0 copy-start.2
  23.8 3.0 %join.2 = (f32[128,128]{1,0:T(8,128)S(1)}, s32[128,128]{1,0:T(8,128)S(1)}, s32[1]{0:T(128)}) custom-call(f32[512,128]{1,0:T(8,128)S(1)} %bitcast.20), custom_call_target="tpu_custom_call" | custom-call | tf_op jit(solution)/shard_map/join/pallas_call | solution.py:590
  26.8 0.0 copy-done.3
  26.8 0.0 copy-done.1
  26.8 0.0 copy-done.2
  26.8 0.9 %while.12 = (s32[]{:T(128)}, f32[128,128]{1,0:T(8,128)S(1)}, s32[128,128]{1,0:T(8,128)S(1)}, s32[1]{0:T(128)}, s32[1]{0:T(128)}, /*index=5*/s32[256,128]{1,0:T(8...) while((s32[]{:T(128)}, f32[128,128]{1,0:T(8,128)S(1)}, s32[128,128]{1,0:T(8,128)S(1)}, ...), condition=%wide.region_1.2_spmd, body=%wide.region_0.1_spmd.sunk | while | flops 98306 | bytes 1310845 | solution.py:602
  27.7 0.0 copy-start
  27.7 0.0 copy-start.4
  27.7 0.6 %copy-done = f32[128,128]{1,0:T(8,128)} copy-done((f32[128,128]{1,0:T(8,128)}, f32[128,128]{1,0:T(8,128)S(1)}, u32[]{:S(2)}) %copy-start) | copy-done | bytes 65560
  28.3 0.0 copy-done.4
Async XLA Ops:
  6.2 20.6 %copy-start.3 = (f32[32768]{0:T(1024)S(1)}, f32[32768]{0:T(1024)}, u32[]{:S(2)}) copy-start(f32[32768]{0:T(1024)} %param.7) | copy-start | bytes 393220
  6.2 17.6 %all-to-all-start.1 = ((f32[32,16,128]{2,1,0:T(8,128)}), f32[32,16,128]{2,1,0:T(8,128)S(1)}, u32[]{:S(2)}, u32[]{:S(2)}) async-start(f32[32,16,128]{2,1,0:T(8,128)} %bitcast.8), calls=%async_computation.1 | async-start | bytes 524288 | tf_op jit(solution)/shard_map/all_to_all | solution.py:589
  23.8 3.0 %copy-start.1 = (s32[32768]{0:T(1024)S(1)}, s32[32768]{0:T(1024)}, u32[]{:S(2)}) copy-start(s32[32768]{0:T(1024)} %param.5) | copy-start | bytes 393220
  23.8 3.0 %copy-start.2 = (s32[32768]{0:T(1024)S(1)}, s32[32768]{0:T(1024)}, u32[]{:S(2)}) copy-start(s32[32768]{0:T(1024)} %param.6) | copy-start | bytes 393220
  27.7 0.6 %copy-start = (f32[128,128]{1,0:T(8,128)}, f32[128,128]{1,0:T(8,128)S(1)}, u32[]{:S(2)}) copy-start(f32[128,128]{1,0:T(8,128)S(1)} %get-tuple-element.54) | copy-start | bytes 196612
  27.7 0.6 %copy-start.4 = (s32[128,128]{1,0:T(8,128)}, s32[128,128]{1,0:T(8,128)S(1)}, u32[]{:S(2)}) copy-start(s32[128,128]{1,0:T(8,128)S(1)} %get-tuple-element.55) | copy-start | bytes 196612

commit v5 on v4

--- a/solution.py
+++ b/solution.py
@@ -388,7 +388,7 @@
     return sizes
 
 
-def split_kernel(own, slots, chunk, round_ref, odd_ref, cell_in, vehicle_in, speed_in, out_hbm, cell_ref, vehicle_ref, speed_ref, out_ref, low_ref, high_ref, cell_pad, key_pad, in_sem, out_sem):
+def split_kernel(own, slots, chunk, round_ref, odd_ref, cell_in, vehicle_in, speed_in, out_ref, cell_ref, vehicle_ref, speed_ref, low_ref, high_ref, cell_pad, key_pad, in_sem):
     n = CELLS // own
     count = cell_ref.shape[0] // ROWS
     bits = (count * TILE).bit_length() - 1
@@ -436,16 +436,7 @@
     sub, lane = sub_iota(), lane_iota()
     skip = round_ref[0] * (slots * LANES)
     base = jnp.int32(0)
-    group = n // 4
-    writes = []
-    for k in range(4):
-        part = pl.ds(jnp.where(odd == 1, 3 - k, k) * (group * chunk), group * chunk)
-        writes.append(
-            pltpu.make_async_copy(out_ref.at[part, :], out_hbm.at[part, :], out_sem.at[k])
-        )
     for o in range(n):
-        if o % group == 0 and o > group:
-            writes[o // group - 2].start()
         start = base + skip
         valid = sub * LANES + lane < sizes[o] - skip
         start = jnp.minimum(start, count * TILE)
@@ -467,10 +458,6 @@
         tail = chunk - 3 * slots
         fill = jnp.full((tail, LANES), most.astype(jnp.float32))
         out_ref[pl.ds(target + 3 * slots, tail), :] = fill
-    for k in (2, 3):
-        writes[k].start()
-    for write in writes:
-        write.wait()
 
 
 def join_kernel(own, n, slots, chunk, in_ref, speed_ref, ident_ref, rounds_ref, cell_pad, key_pad):
@@ -554,19 +541,18 @@
 
     split = pl.pallas_call(
         functools.partial(split_kernel, own, slots, chunk),
-        out_shape=jax.ShapeDtypeStruct((n * chunk, LANES), jnp.float32),
+        out_shape=pltpu.VMEM((n * chunk, LANES), jnp.float32),
         in_specs=[smem, smem, hbm, hbm, hbm],
-        out_specs=hbm,
+        out_specs=vmem,
         scratch_shapes=[
             pltpu.VMEM((rows, LANES), jnp.int32),
             pltpu.VMEM((rows, LANES), jnp.int32),
             pltpu.VMEM((rows, LANES), jnp.float32),
-            pltpu.VMEM((n * chunk, LANES), jnp.float32),
             pltpu.VMEM((rows + ROWS, LANES), jnp.int32),
             pltpu.VMEM((rows + ROWS, LANES), jnp.int32),
         ]
         + pads(rows)
-        + [pltpu.SemaphoreType.DMA((rows // LANES, 3)), pltpu.SemaphoreType.DMA((4,))],
+        + [pltpu.SemaphoreType.DMA((rows // LANES, 3))],
         compiler_params=params,
         name="split",
     )
@@ -599,9 +585,11 @@
         )
         return index + 1, jnp.maximum(best, more), ident
 
-    _, best, ident = lax.while_loop(
-        lambda state: state[0] < rounds[0], again, (jnp.int32(1), best, ident)
-    )
+    def rest(best, ident):
+        state = (jnp.int32(1), best, ident)
+        return lax.while_loop(lambda state: state[0] < rounds[0], again, state)[1:]
+
+    best, ident = lax.cond(rounds[0] > 1, rest, lambda *kept: kept, best, ident)
     return best.reshape(own), ident.reshape(own)
 
 

time: 28.6 us -> 27.8 us (0.972)
  blocking collectives: 0 us -> 17.4 us
  waiting for transfers between devices: 10.3 us -> 0 us
  starting transfers between devices: 7.33 us -> 0 us
  between operations: 0.72 us -> 1.5 us
  local copies, waits for them, and re-layouts: 0.65 us -> 0.01 us
  loops' own time: 0.86 us -> 0.23 us
    all_to_all x0 -> x1, blocking collectives: none -> 17.4 us  [one_round(): got = lax.all_to_all(sent.reshape(n, chunk, LANES), AXES, 0, 0, tiled=True)]
    all_to_all x1 -> x0, waiting for transfers between devices: 10.3 us -> none  [one_round(): got = lax.all_to_all(sent.reshape(n, chunk, LANES), AXES, 0, 0, tiled=True)]
    all_to_all x1 -> x0, starting transfers between devices: 7.33 us -> none  [one_round(): got = lax.all_to_all(sent.reshape(n, chunk, LANES), AXES, 0, 0, tiled=True)]
    pallas_call x1, Pallas kernels: 5.58 us -> 4.86 us  [one_round(): sent = split(index.reshape(1), odd, *inputs)]
    pallas_call x1, Pallas kernels: 2.96 us -> 3.61 us  [one_round(): return join(got.reshape(n * chunk, LANES))]
    unnamed x10 -> x6, local copies, waits for them, and re-layouts: 0.65 us -> 0.01 us
    another operation x1, loops' own time: 0.86 us -> 0.23 us  [per_device(): best, ident = lax.cond(rounds[0] > 1, rest, lambda *kept: kept, best, ident)]
  transfers between devices with their start and end apart: 1 -> 0, of which waited for: 1 -> 0; matrix products, arithmetic and copies ran while one was open for 0% -> 0% of each run, Pallas kernels for 0% -> 0%
where the time goes in v5:
time: 27.8 us; the launch traced here: 27.6 us
  blocking collectives  17.4 us (63%)
  Pallas kernels  8.46 us (30%)
  between operations  1.5 us (5%)
    all_to_all x1, blocking collectives, one_round(): got = lax.all_to_all(sent.reshape(n, chunk, LANES), AXES, 0, 0, tiled=True)  17.4 us
    pallas_call x1, Pallas kernels, one_round(): sent = split(index.reshape(1), odd, *inputs)  4.86 us
    pallas_call x1, Pallas kernels, one_round(): return join(got.reshape(n * chunk, LANES))  3.61 us

profile of v5, /device:TPU:0, one launch (start us, length us, event | category | flops | bytes accessed | tf_op | source)
XLA Modules:
  0.0 27.6 jit_solution(7148262610020134023)
XLA Ops:
  0.6 4.9 %split.2 = f32[512,128]{1,0:T(8,128)S(1)} custom-call(s32[1]{0:T(128)} %constant.6.clone.1.round_ref, s32[1]{0:T(128)} %bitcast.8.odd_ref, s32[256,128]{1,0:T(8,128)} %bitcast.27, s32[256,128]{1,0:T(8,128)} %bitcast.29, f32[256,128]{1,0:T(8,128)} %bitcast.31), custom_call_target="tpu_custom_call" | custom-call | tf_op jit(solution)/shard_map/split/pallas_call | solution.py:574
  5.5 0.0 copy-start.3
  5.5 17.4 %all_to_all.11 = f32[32,16,128]{2,1,0:T(8,128)S(1)} all-to-all(f32[32,16,128]{2,1,0:T(8,128)S(1)} %bitcast.23), channel_id=1, replica_groups=mesh['gx'=2,'gy'=16] {'gx','gy'}, dimensions={0} | all-to-all | bytes 524288 | tf_op jit(solution)/shard_map/all_to_all | solution.py:575
  22.9 0.0 copy-start.1
  22.9 0.0 copy-start.2
  22.9 3.6 %join.2 = (f32[128,128]{1,0:T(8,128)}, s32[128,128]{1,0:T(8,128)}, s32[1]{0:T(128)}) custom-call(f32[512,128]{1,0:T(8,128)S(1)} %bitcast.24), custom_call_target="tpu_custom_call" | custom-call | tf_op jit(solution)/shard_map/join/pallas_call | solution.py:576
  27.2 0.0 copy-done.3
  27.2 0.0 copy-done.1
  27.2 0.0 copy-done.2
  27.2 0.2 conditional.1
Async XLA Ops:
  5.5 21.7 %copy-start.3 = (f32[32768]{0:T(1024)S(1)}, f32[32768]{0:T(1024)}, u32[]{:S(2)}) copy-start(f32[32768]{0:T(1024)} %param.9) | copy-start | bytes 393220
  22.9 4.3 %copy-start.1 = (s32[32768]{0:T(1024)S(1)}, s32[32768]{0:T(1024)}, u32[]{:S(2)}) copy-start(s32[32768]{0:T(1024)} %param.7) | copy-start | bytes 393220
  22.9 4.3 %copy-start.2 = (s32[32768]{0:T(1024)S(1)}, s32[32768]{0:T(1024)}, u32[]{:S(2)}) copy-start(s32[32768]{0:T(1024)} %param.8) | copy-start | bytes 393220

commit v6 on v5

--- a/solution.py
+++ b/solution.py
@@ -106,6 +106,9 @@
         if self.load is not None:
             self.keys, self.loads = self.load()
             self.load = None
+        if levels[0] >= 15 and self.index:
+            late = jnp.where(self.before.loads[15] > 1 << 30, 1, 0)
+            self.keys = [x + late for x in self.keys]
         for level in levels:
             if level < 15:
                 self.face(level if level < bits else None)
@@ -141,6 +144,8 @@
                 if other is not one:
                     for g in range(16):
                         exchange(one.keys, one.loads, g, g, other.keys, other.loads)
+        for block in blocks[1:]:
+            block.before = blocks[block.index - 1]
         run_all(block.levels([level], bits) for block in blocks)
     keys = sum((block.keys for block in blocks), [])
     return keys, sum((block.loads for block in blocks), [])

time: 27.8 us -> 27.8 us (level)
  no operation moved by 1% of the time
where the time goes in v6:
time: 27.8 us; the launch traced here: 27.6 us
  blocking collectives  17.4 us (63%)
  Pallas kernels  8.5 us (31%)
  between operations  1.5 us (5%)
    all_to_all x1, blocking collectives, one_round(): got = lax.all_to_all(sent.reshape(n, chunk, LANES), AXES, 0, 0, tiled=True)  17.4 us
    pallas_call x1, Pallas kernels, one_round(): sent = split(index.reshape(1), odd, *inputs)  4.86 us
    pallas_call x1, Pallas kernels, one_round(): return join(got.reshape(n * chunk, LANES))  3.64 us

profile of v6, /device:TPU:0, one launch (start us, length us, event | category | flops | bytes accessed | tf_op | source)
XLA Modules:
  0.0 27.6 jit_solution(9911865203385864035)
XLA Ops:
  0.6 4.9 %split.2 = f32[512,128]{1,0:T(8,128)S(1)} custom-call(s32[1]{0:T(128)} %constant.6.clone.1.round_ref, s32[1]{0:T(128)} %bitcast.8.odd_ref, s32[256,128]{1,0:T(8,128)} %bitcast.27, s32[256,128]{1,0:T(8,128)} %bitcast.29, f32[256,128]{1,0:T(8,128)} %bitcast.31), custom_call_target="tpu_custom_call" | custom-call | tf_op jit(solution)/shard_map/split/pallas_call | solution.py:579
  5.5 0.0 copy-start.3
  5.5 17.4 %all_to_all.11 = f32[32,16,128]{2,1,0:T(8,128)S(1)} all-to-all(f32[32,16,128]{2,1,0:T(8,128)S(1)} %bitcast.23), channel_id=1, replica_groups=mesh['gx'=2,'gy'=16] {'gx','gy'}, dimensions={0} | all-to-all | bytes 524288 | tf_op jit(solution)/shard_map/all_to_all | solution.py:580
  22.9 0.0 copy-start.1
  22.9 0.0 copy-start.2
  22.9 3.6 %join.2 = (f32[128,128]{1,0:T(8,128)}, s32[128,128]{1,0:T(8,128)}, s32[1]{0:T(128)}) custom-call(f32[512,128]{1,0:T(8,128)S(1)} %bitcast.24), custom_call_target="tpu_custom_call" | custom-call | tf_op jit(solution)/shard_map/join/pallas_call | solution.py:581
  27.2 0.0 copy-done.3
  27.2 0.0 copy-done.1
  27.2 0.0 copy-done.2
  27.2 0.2 conditional.1
Async XLA Ops:
  5.5 21.7 %copy-start.3 = (f32[32768]{0:T(1024)S(1)}, f32[32768]{0:T(1024)}, u32[]{:S(2)}) copy-start(f32[32768]{0:T(1024)} %param.9) | copy-start | bytes 393220
  22.9 4.3 %copy-start.1 = (s32[32768]{0:T(1024)S(1)}, s32[32768]{0:T(1024)}, u32[]{:S(2)}) copy-start(s32[32768]{0:T(1024)} %param.7) | copy-start | bytes 393220
  22.9 4.3 %copy-start.2 = (s32[32768]{0:T(1024)S(1)}, s32[32768]{0:T(1024)}, u32[]{:S(2)}) copy-start(s32[32768]{0:T(1024)} %param.8) | copy-start | bytes 393220
